TPU v7x, 64 devices: a 2x2x8 block of a 4x4x8 slice. The times are simulated.
64 devices in a mesh: dp: 4 (over x, y), cp: 16 (over z, core).
Axes of the slice: x: 2, y: 2, z: 8, core: 2. Of those that a mesh axis runs over, the one named last changes fastest.
The devices are a block of a 4x4x8 slice.
Arguments:
- q_tok: bfloat16 [32768, 8, 128], P(('dp', 'cp')), parts along dimension 0
- k_tok: bfloat16 [32768, 128], P(('dp', 'cp')), parts along dimension 0
- v_tok: bfloat16 [32768, 128], P(('dp', 'cp')), parts along dimension 0
- fwd_out: bfloat16 [32768, 8, 128], P(('dp', 'cp')), parts along dimension 0
- d_out: bfloat16 [32768, 8, 128], P(('dp', 'cp')), parts along dimension 0
- lse_row: float32 [32768, 8], P(('dp', 'cp')), parts along dimension 0
Outputs:
- output 1: bfloat16 [32768, 8, 128], P(('dp', 'cp')), parts along dimension 0
- output 2: bfloat16 [32768, 128], P(('dp', 'cp')), parts along dimension 0
- output 3: bfloat16 [32768, 128], P(('dp', 'cp')), parts along dimension 0
There are 4 independent parts. A program takes and returns all parts, laid end to end along the dimension named above; each array names one.
All inputs are finite; a program needn't handle non-finite values.
Results may differ from a plain program's by a relative error of at most 0.001.
Values are sent between devices in bfloat16 or wider.
A program may use at most 768 MiB of HBM per device.

v0:
```python
import jax
import jax.numpy as jnp
from jax import lax
from jax.sharding import PartitionSpec as P


def pair_scores(q_block, do_block, lse_block, delta_block, k_block, v_block, on_diag, softmax_scale):
    logits = jnp.einsum('rgd,cd->rgc', q_block, k_block, preferred_element_type=jnp.float32)
    row_ids = jnp.arange(q_block.shape[0])
    allowed = jnp.logical_or(row_ids[None, :] <= row_ids[:, None], jnp.logical_not(on_diag))
    prob_mat = jnp.exp(jnp.where(allowed[:, None, :], logits * softmax_scale - lse_block[:, :, None], -jnp.inf))
    d_prob = jnp.einsum('rgd,cd->rgc', do_block, v_block, preferred_element_type=jnp.float32)
    d_score = (prob_mat * (d_prob - delta_block[:, :, None])).astype(jnp.bfloat16)
    return prob_mat.astype(jnp.bfloat16), d_score


def solution(mesh):
    n_dev = mesh.shape['cp']
    forward_perm = [(i, (i + 1) % n_dev) for i in range(n_dev)]
    row_spec = P(('dp', 'cp'))

    def local_fn(q_tok, k_tok, v_tok, fwd_out, d_out, lse_row):
        softmax_scale = q_tok.shape[-1] ** -0.5
        my_index = lax.axis_index('cp')
        row_delta = jnp.einsum('rgd,rgd->rg', d_out, fwd_out, preferred_element_type=jnp.float32)

        def accumulate(step, state):
            def pair_update(state_in):
                dq_acc, k_cur, v_cur, dk_acc, dv_acc = state_in
                prob_low, score_low = pair_scores(q_tok, d_out, lse_row, row_delta, k_cur, v_cur, step == 0, softmax_scale)
                dq_acc = dq_acc + jnp.einsum('rgc,cd->rgd', score_low, k_cur, preferred_element_type=jnp.float32)
                dk_acc = dk_acc + jnp.einsum('rgc,rgd->cd', score_low, q_tok, preferred_element_type=jnp.float32)
                dv_acc = dv_acc + jnp.einsum('rgc,rgd->cd', prob_low, d_out, preferred_element_type=jnp.float32)
                return (dq_acc, k_cur, v_cur, dk_acc, dv_acc)

            def keep_state(state_in):
                return state_in

            return lax.cond(step <= my_index, pair_update, keep_state, state)

        def step_fn(step, state):
            dq_acc, k_cur, v_cur, dk_acc, dv_acc = accumulate(step, state)
            k_next = lax.ppermute(k_cur, 'cp', forward_perm)
            v_next = lax.ppermute(v_cur, 'cp', forward_perm)
            dk_next = lax.ppermute(dk_acc, 'cp', forward_perm)
            dv_next = lax.ppermute(dv_acc, 'cp', forward_perm)
            return (dq_acc, k_next, v_next, dk_next, dv_next)

        kv_zeros = jnp.zeros(k_tok.shape, jnp.float32)
        state = (jnp.zeros(q_tok.shape, jnp.float32), k_tok, v_tok, kv_zeros, kv_zeros)
        state = lax.fori_loop(0, n_dev - 1, step_fn, state)
        dq_acc, k_cur, v_cur, dk_acc, dv_acc = accumulate(n_dev - 1, state)
        dk_home = lax.ppermute(dk_acc, 'cp', forward_perm)
        dv_home = lax.ppermute(dv_acc, 'cp', forward_perm)
        grad_q = (dq_acc * softmax_scale).astype(jnp.bfloat16)
        grad_k = (dk_home * softmax_scale).astype(jnp.bfloat16)
        grad_v = dv_home.astype(jnp.bfloat16)
        return grad_q, grad_k, grad_v

    return jax.shard_map(local_fn, mesh=mesh, in_specs=(row_spec, row_spec, row_spec, row_spec, row_spec, row_spec), out_specs=(row_spec, row_spec, row_spec), check_vma=False)
```

profile of v0, /device:TPU:30, one launch (start us, length us, event | category | flops | bytes accessed | tf_op | source)
XLA Modules:
  0.0 418.1 jit_solution(7257864035742019327)
XLA Ops:
  9.5 383.8 %while.21 = (s32[]{:T(128)}, f32[512,8,128]{2,0,1:T(8,128)S(1)}, bf16[512,128]{1,0:T(8,128)(2,1)}, bf16[512,128]{1,0:T(8,128)(2,1)}, f32[512,128]{1,0:T(8,128)S(...) while((s32[]{:T(128)}, f32[512,8,128]{2,0,1:T(8,128)S(1)}, ...), condition=%wide.region_3.4_spmd, body=%wide.region_0.3_spmd.sunk | while | flops 2706505728 | bytes 57917960 | solution.py:51
  12.0 11.8 %conditional.4 = ((f32[512,8,128]{2,0,1:T(8,128)S(1)}, f32[512,128]{1,0:T(8,128)S(1)}, f32[512,128]{1,0:T(8,128)})) conditional(s32[]{:T(128)} %convert_element_type.52, (f32[512,8,128]{2,0,1:T(8,128)S(1)}, f32[512,128]{1,0:T(8,128)S(1)}, f32[512,128]{1,0:T(8,128)}) %tuple.54, (s32[]{:T(128)}, bf16[512,8,128]{2,0,1:T(8,128)(2,1)S(1)}, ...), branch_computations={%region_1.0_spmd, %region_2.2_spmd} | conditional | flops 2706505728 | bytes 53198976 | solution.py:39
  13.4 4.6 %fusion.7 = f32[512,128]{1,0:T(8,128)} fusion(f32[512,128]{1,0:T(8,128)} %get-tuple-element.232, bf16[512,8,128]{2,0,1:T(8,128)(2,1)S(1)} %copy-done.4, f32[512,8,512]{2,0,1:T(8,128)S(1)} %fusion.14, f32[512,8]{0,1:T(8,128)S(1)} %copy-done.5, pred[512,512]{1,0:T(8,128)(4,1)S(1)} %fusion.11), kind=kOutput, calls=%fused_computation.8 | convolution fusion | flops 545325056 | bytes 10240000 | tf_op jit(solution)/shard_map/while/body/eval_jaxpr/cond/branch_1_fun/rgc,rgd->cd/dot_general | solution.py:33
  18.0 3.1 multiply_convert_fusion
  28.3 6.4 %collective-permute-done.2 = f32[512,128]{1,0:T(8,128)} collective-permute-done((f32[512,128]{1,0:T(8,128)S(1)}, f32[512,128]{1,0:T(8,128)}, u32[]{:S(2)}, u32[]{:S(2)}) %collective-permute-start.2) | collective-permute-done | bytes 262176 | tf_op jit(solution)/shard_map/while/body/eval_jaxpr/ppermute | solution.py:45
  42.8 6.5 %collective-permute-start.2 = (f32[512,128]{1,0:T(8,128)S(1)}, f32[512,128]{1,0:T(8,128)}, u32[]{:S(2)}, u32[]{:S(2)}) collective-permute-start(f32[512,128]{1,0:T(8,128)S(1)} %get-tuple-element.393), channel_id=1, source_target_pairs={{0,1},{1,2},{2,3},{3,4},{4,5},{5,6},{6,7},{7,8},{8,9},{9,10},{10,1... | collective-permute-start | bytes 786440 | tf_op jit(solution)/shard_map/while/body/eval_jaxpr/ppermute | solution.py:45
  54.0 3.9 collective-permute-done.2
  66.0 11.5 %collective-permute-start.3 = (f32[512,128]{1,0:T(8,128)}, f32[512,128]{1,0:T(8,128)}, u32[]{:S(2)}, u32[]{:S(2)}) collective-permute-start(f32[512,128]{1,0:T(8,128)} %get-tuple-element.394), channel_id=1, source_target_pairs={{0,1},{1,2},{2,3},{3,4},{4,5},{5,6},{6,7},{7,8},{8,9},{9,10},{10,1... | collective-permute-start | bytes 786440 | tf_op jit(solution)/shard_map/while/body/eval_jaxpr/ppermute | solution.py:46
  91.4 11.6 %collective-permute-start = (bf16[512,128]{1,0:T(8,128)(2,1)S(1)}, bf16[512,128]{1,0:T(8,128)(2,1)}, u32[]{:S(2)}, u32[]{:S(2)}) collective-permute-start(bf16[512,128]{1,0:T(8,128)(2,1)S(1)} %copy.52), channel_id=1, source_target_pairs={{0,1},{1,2},{2,3},{3,4},{4,5},{5,6},{6,7},{7,8},{8,9},{9,10},{10,1... | collective-permute-start | bytes 393224 | tf_op jit(solution)/shard_map/while/body/eval_jaxpr/ppermute | solution.py:43
  116.9 14.9 %collective-permute-start.1 = (bf16[512,128]{1,0:T(8,128)(2,1)}, bf16[512,128]{1,0:T(8,128)(2,1)}, u32[]{:S(2)}, u32[]{:S(2)}) collective-permute-start(bf16[512,128]{1,0:T(8,128)(2,1)} %copy.53), channel_id=1, source_target_pairs={{0,1},{1,2},{2,3},{3,4},{4,5},{5,6},{6,7},{7,8},{8,9},{9,10},{10,1... | collective-permute-start | bytes 393224 | tf_op jit(solution)/shard_map/while/body/eval_jaxpr/ppermute | solution.py:44
  140.0 3.1 collective-permute-start
  143.1 3.7 collective-permute-start.1
  146.8 9.3 %collective-permute-done.2 = f32[512,128]{1,0:T(8,128)} collective-permute-done((f32[512,128]{1,0:T(8,128)S(1)}, f32[512,128]{1,0:T(8,128)}, u32[]{:S(2)}, u32[]{:S(2)}) %collective-permute-start.2) | collective-permute-done | bytes 262176 | tf_op jit(solution)/shard_map/while/body/eval_jaxpr/ppermute | solution.py:45
  166.9 3.1 collective-permute-start
  170.1 3.7 collective-permute-start.1
  173.8 8.1 %collective-permute-done.2 = f32[512,128]{1,0:T(8,128)} collective-permute-done((f32[512,128]{1,0:T(8,128)S(1)}, f32[512,128]{1,0:T(8,128)}, u32[]{:S(2)}, u32[]{:S(2)}) %collective-permute-start.2) | collective-permute-done | bytes 262176 | tf_op jit(solution)/shard_map/while/body/eval_jaxpr/ppermute | solution.py:45
  189.9 3.9 collective-permute-start.3
  193.9 3.1 collective-permute-start
  197.0 3.7 collective-permute-start.1
  200.7 6.9 %collective-permute-done.2 = f32[512,128]{1,0:T(8,128)} collective-permute-done((f32[512,128]{1,0:T(8,128)S(1)}, f32[512,128]{1,0:T(8,128)}, u32[]{:S(2)}, u32[]{:S(2)}) %collective-permute-start.2) | collective-permute-done | bytes 262176 | tf_op jit(solution)/shard_map/while/body/eval_jaxpr/ppermute | solution.py:45
  215.7 8.3 %collective-permute-start = (bf16[512,128]{1,0:T(8,128)(2,1)S(1)}, bf16[512,128]{1,0:T(8,128)(2,1)}, u32[]{:S(2)}, u32[]{:S(2)}) collective-permute-start(bf16[512,128]{1,0:T(8,128)(2,1)S(1)} %copy.52), channel_id=1, source_target_pairs={{0,1},{1,2},{2,3},{3,4},{4,5},{5,6},{6,7},{7,8},{8,9},{9,10},{10,1... | collective-permute-start | bytes 393224 | tf_op jit(solution)/shard_map/while/body/eval_jaxpr/ppermute | solution.py:43
  223.9 3.7 collective-permute-start.1
  227.6 5.6 %collective-permute-done.2 = f32[512,128]{1,0:T(8,128)} collective-permute-done((f32[512,128]{1,0:T(8,128)S(1)}, f32[512,128]{1,0:T(8,128)}, u32[]{:S(2)}, u32[]{:S(2)}) %collective-permute-start.2) | collective-permute-done | bytes 262176 | tf_op jit(solution)/shard_map/while/body/eval_jaxpr/ppermute | solution.py:45
  241.4 13.2 %collective-permute-start.1 = (bf16[512,128]{1,0:T(8,128)(2,1)}, bf16[512,128]{1,0:T(8,128)(2,1)}, u32[]{:S(2)}, u32[]{:S(2)}) collective-permute-start(bf16[512,128]{1,0:T(8,128)(2,1)} %copy.53), channel_id=1, source_target_pairs={{0,1},{1,2},{2,3},{3,4},{4,5},{5,6},{6,7},{7,8},{8,9},{9,10},{10,1... | collective-permute-start | bytes 393224 | tf_op jit(solution)/shard_map/while/body/eval_jaxpr/ppermute | solution.py:44
  254.6 4.4 %collective-permute-done.2 = f32[512,128]{1,0:T(8,128)} collective-permute-done((f32[512,128]{1,0:T(8,128)S(1)}, f32[512,128]{1,0:T(8,128)}, u32[]{:S(2)}, u32[]{:S(2)}) %collective-permute-start.2) | collective-permute-done | bytes 262176 | tf_op jit(solution)/shard_map/while/body/eval_jaxpr/ppermute | solution.py:45
  269.7 15.1 %collective-permute-done.2 = f32[512,128]{1,0:T(8,128)} collective-permute-done((f32[512,128]{1,0:T(8,128)S(1)}, f32[512,128]{1,0:T(8,128)}, u32[]{:S(2)}, u32[]{:S(2)}) %collective-permute-start.2) | collective-permute-done | bytes 262176 | tf_op jit(solution)/shard_map/while/body/eval_jaxpr/ppermute | solution.py:45
  292.9 17.5 %collective-permute-done.2 = f32[512,128]{1,0:T(8,128)} collective-permute-done((f32[512,128]{1,0:T(8,128)S(1)}, f32[512,128]{1,0:T(8,128)}, u32[]{:S(2)}, u32[]{:S(2)}) %collective-permute-start.2) | collective-permute-done | bytes 262176 | tf_op jit(solution)/shard_map/while/body/eval_jaxpr/ppermute | solution.py:45
  318.7 17.5 %collective-permute-done.2 = f32[512,128]{1,0:T(8,128)} collective-permute-done((f32[512,128]{1,0:T(8,128)S(1)}, f32[512,128]{1,0:T(8,128)}, u32[]{:S(2)}, u32[]{:S(2)}) %collective-permute-start.2) | collective-permute-done | bytes 262176 | tf_op jit(solution)/shard_map/while/body/eval_jaxpr/ppermute | solution.py:45
  344.4 17.5 %collective-permute-done.2 = f32[512,128]{1,0:T(8,128)} collective-permute-done((f32[512,128]{1,0:T(8,128)S(1)}, f32[512,128]{1,0:T(8,128)}, u32[]{:S(2)}, u32[]{:S(2)}) %collective-permute-start.2) | collective-permute-done | bytes 262176 | tf_op jit(solution)/shard_map/while/body/eval_jaxpr/ppermute | solution.py:45
  370.1 17.5 %collective-permute-done.2 = f32[512,128]{1,0:T(8,128)} collective-permute-done((f32[512,128]{1,0:T(8,128)S(1)}, f32[512,128]{1,0:T(8,128)}, u32[]{:S(2)}, u32[]{:S(2)}) %collective-permute-start.2) | collective-permute-done | bytes 262176 | tf_op jit(solution)/shard_map/while/body/eval_jaxpr/ppermute | solution.py:45
  396.9 17.0 %collective-permute-done.5 = bf16[512,128]{1,0:T(8,128)(2,1)S(1)} collective-permute-done((bf16[512,128]{1,0:T(8,128)(2,1)S(1)}, bf16[512,128]{1,0:T(8,128)(2,1)S(1)}, u32[]{:S(2)}, u32[]{:S(2)}) %collective-permute-start.5) | collective-permute-done | bytes 131104 | tf_op jit(solution)/shard_map/ppermute | solution.py:54
  414.0 2.8 collective-permute-done.4
  (197 shorter events, 167.0 us)
Async XLA Ops:
  112.7 19.0 %collective-permute-start.2 = (f32[512,128]{1,0:T(8,128)S(1)}, f32[512,128]{1,0:T(8,128)}, u32[]{:S(2)}, u32[]{:S(2)}) collective-permute-start(f32[512,128]{1,0:T(8,128)S(1)} %get-tuple-element.393), channel_id=1, source_target_pairs={{0,1},{1,2},{2,3},{3,4},{4,5},{5,6},{6,7},{7,8},{8,9},{9,10},{10,1... | collective-permute-start | bytes 786440 | tf_op jit(solution)/shard_map/while/body/eval_jaxpr/ppermute | solution.py:45
  112.8 20.4 %collective-permute-start.3 = (f32[512,128]{1,0:T(8,128)}, f32[512,128]{1,0:T(8,128)}, u32[]{:S(2)}, u32[]{:S(2)}) collective-permute-start(f32[512,128]{1,0:T(8,128)} %get-tuple-element.394), channel_id=1, source_target_pairs={{0,1},{1,2},{2,3},{3,4},{4,5},{5,6},{6,7},{7,8},{8,9},{9,10},{10,1... | collective-permute-start | bytes 786440 | tf_op jit(solution)/shard_map/while/body/eval_jaxpr/ppermute | solution.py:46
  114.1 20.8 %collective-permute-start = (bf16[512,128]{1,0:T(8,128)(2,1)S(1)}, bf16[512,128]{1,0:T(8,128)(2,1)}, u32[]{:S(2)}, u32[]{:S(2)}) collective-permute-start(bf16[512,128]{1,0:T(8,128)(2,1)S(1)} %copy.52), channel_id=1, source_target_pairs={{0,1},{1,2},{2,3},{3,4},{4,5},{5,6},{6,7},{7,8},{8,9},{9,10},{10,1... | collective-permute-start | bytes 393224 | tf_op jit(solution)/shard_map/while/body/eval_jaxpr/ppermute | solution.py:43
  116.9 19.1 %collective-permute-start.1 = (bf16[512,128]{1,0:T(8,128)(2,1)}, bf16[512,128]{1,0:T(8,128)(2,1)}, u32[]{:S(2)}, u32[]{:S(2)}) collective-permute-start(bf16[512,128]{1,0:T(8,128)(2,1)} %copy.53), channel_id=1, source_target_pairs={{0,1},{1,2},{2,3},{3,4},{4,5},{5,6},{6,7},{7,8},{8,9},{9,10},{10,1... | collective-permute-start | bytes 393224 | tf_op jit(solution)/shard_map/while/body/eval_jaxpr/ppermute | solution.py:44
  138.5 20.4 %collective-permute-start.3 = (f32[512,128]{1,0:T(8,128)}, f32[512,128]{1,0:T(8,128)}, u32[]{:S(2)}, u32[]{:S(2)}) collective-permute-start(f32[512,128]{1,0:T(8,128)} %get-tuple-element.394), channel_id=1, source_target_pairs={{0,1},{1,2},{2,3},{3,4},{4,5},{5,6},{6,7},{7,8},{8,9},{9,10},{10,1... | collective-permute-start | bytes 786440 | tf_op jit(solution)/shard_map/while/body/eval_jaxpr/ppermute | solution.py:46
  140.0 20.6 %collective-permute-start = (bf16[512,128]{1,0:T(8,128)(2,1)S(1)}, bf16[512,128]{1,0:T(8,128)(2,1)}, u32[]{:S(2)}, u32[]{:S(2)}) collective-permute-start(bf16[512,128]{1,0:T(8,128)(2,1)S(1)} %copy.52), channel_id=1, source_target_pairs={{0,1},{1,2},{2,3},{3,4},{4,5},{5,6},{6,7},{7,8},{8,9},{9,10},{10,1... | collective-permute-start | bytes 393224 | tf_op jit(solution)/shard_map/while/body/eval_jaxpr/ppermute | solution.py:43
  143.1 18.6 %collective-permute-start.1 = (bf16[512,128]{1,0:T(8,128)(2,1)}, bf16[512,128]{1,0:T(8,128)(2,1)}, u32[]{:S(2)}, u32[]{:S(2)}) collective-permute-start(bf16[512,128]{1,0:T(8,128)(2,1)} %copy.53), channel_id=1, source_target_pairs={{0,1},{1,2},{2,3},{3,4},{4,5},{5,6},{6,7},{7,8},{8,9},{9,10},{10,1... | collective-permute-start | bytes 393224 | tf_op jit(solution)/shard_map/while/body/eval_jaxpr/ppermute | solution.py:44
  164.4 20.2 %collective-permute-start.3 = (f32[512,128]{1,0:T(8,128)}, f32[512,128]{1,0:T(8,128)}, u32[]{:S(2)}, u32[]{:S(2)}) collective-permute-start(f32[512,128]{1,0:T(8,128)} %get-tuple-element.394), channel_id=1, source_target_pairs={{0,1},{1,2},{2,3},{3,4},{4,5},{5,6},{6,7},{7,8},{8,9},{9,10},{10,1... | collective-permute-start | bytes 786440 | tf_op jit(solution)/shard_map/while/body/eval_jaxpr/ppermute | solution.py:46
  166.9 19.4 %collective-permute-start = (bf16[512,128]{1,0:T(8,128)(2,1)S(1)}, bf16[512,128]{1,0:T(8,128)(2,1)}, u32[]{:S(2)}, u32[]{:S(2)}) collective-permute-start(bf16[512,128]{1,0:T(8,128)(2,1)S(1)} %copy.52), channel_id=1, source_target_pairs={{0,1},{1,2},{2,3},{3,4},{4,5},{5,6},{6,7},{7,8},{8,9},{9,10},{10,1... | collective-permute-start | bytes 393224 | tf_op jit(solution)/shard_map/while/body/eval_jaxpr/ppermute | solution.py:43
  189.9 20.4 %collective-permute-start.3 = (f32[512,128]{1,0:T(8,128)}, f32[512,128]{1,0:T(8,128)}, u32[]{:S(2)}, u32[]{:S(2)}) collective-permute-start(f32[512,128]{1,0:T(8,128)} %get-tuple-element.394), channel_id=1, source_target_pairs={{0,1},{1,2},{2,3},{3,4},{4,5},{5,6},{6,7},{7,8},{8,9},{9,10},{10,1... | collective-permute-start | bytes 786440 | tf_op jit(solution)/shard_map/while/body/eval_jaxpr/ppermute | solution.py:46
  215.7 20.4 %collective-permute-start.3 = (f32[512,128]{1,0:T(8,128)}, f32[512,128]{1,0:T(8,128)}, u32[]{:S(2)}, u32[]{:S(2)}) collective-permute-start(f32[512,128]{1,0:T(8,128)} %get-tuple-element.394), channel_id=1, source_target_pairs={{0,1},{1,2},{2,3},{3,4},{4,5},{5,6},{6,7},{7,8},{8,9},{9,10},{10,1... | collective-permute-start | bytes 786440 | tf_op jit(solution)/shard_map/while/body/eval_jaxpr/ppermute | solution.py:46
  215.7 22.1 %collective-permute-start = (bf16[512,128]{1,0:T(8,128)(2,1)S(1)}, bf16[512,128]{1,0:T(8,128)(2,1)}, u32[]{:S(2)}, u32[]{:S(2)}) collective-permute-start(bf16[512,128]{1,0:T(8,128)(2,1)S(1)} %copy.52), channel_id=1, source_target_pairs={{0,1},{1,2},{2,3},{3,4},{4,5},{5,6},{6,7},{7,8},{8,9},{9,10},{10,1... | collective-permute-start | bytes 393224 | tf_op jit(solution)/shard_map/while/body/eval_jaxpr/ppermute | solution.py:43
  241.4 20.4 %collective-permute-start.3 = (f32[512,128]{1,0:T(8,128)}, f32[512,128]{1,0:T(8,128)}, u32[]{:S(2)}, u32[]{:S(2)}) collective-permute-start(f32[512,128]{1,0:T(8,128)} %get-tuple-element.394), channel_id=1, source_target_pairs={{0,1},{1,2},{2,3},{3,4},{4,5},{5,6},{6,7},{7,8},{8,9},{9,10},{10,1... | collective-permute-start | bytes 786440 | tf_op jit(solution)/shard_map/while/body/eval_jaxpr/ppermute | solution.py:46
  241.4 22.1 %collective-permute-start = (bf16[512,128]{1,0:T(8,128)(2,1)S(1)}, bf16[512,128]{1,0:T(8,128)(2,1)}, u32[]{:S(2)}, u32[]{:S(2)}) collective-permute-start(bf16[512,128]{1,0:T(8,128)(2,1)S(1)} %copy.52), channel_id=1, source_target_pairs={{0,1},{1,2},{2,3},{3,4},{4,5},{5,6},{6,7},{7,8},{8,9},{9,10},{10,1... | collective-permute-start | bytes 393224 | tf_op jit(solution)/shard_map/while/body/eval_jaxpr/ppermute | solution.py:43
  241.4 23.2 %collective-permute-start.1 = (bf16[512,128]{1,0:T(8,128)(2,1)}, bf16[512,128]{1,0:T(8,128)(2,1)}, u32[]{:S(2)}, u32[]{:S(2)}) collective-permute-start(bf16[512,128]{1,0:T(8,128)(2,1)} %copy.53), channel_id=1, source_target_pairs={{0,1},{1,2},{2,3},{3,4},{4,5},{5,6},{6,7},{7,8},{8,9},{9,10},{10,1... | collective-permute-start | bytes 393224 | tf_op jit(solution)/shard_map/while/body/eval_jaxpr/ppermute | solution.py:44
  267.1 20.4 %collective-permute-start.3 = (f32[512,128]{1,0:T(8,128)}, f32[512,128]{1,0:T(8,128)}, u32[]{:S(2)}, u32[]{:S(2)}) collective-permute-start(f32[512,128]{1,0:T(8,128)} %get-tuple-element.394), channel_id=1, source_target_pairs={{0,1},{1,2},{2,3},{3,4},{4,5},{5,6},{6,7},{7,8},{8,9},{9,10},{10,1... | collective-permute-start | bytes 786440 | tf_op jit(solution)/shard_map/while/body/eval_jaxpr/ppermute | solution.py:46
  267.1 22.1 %collective-permute-start = (bf16[512,128]{1,0:T(8,128)(2,1)S(1)}, bf16[512,128]{1,0:T(8,128)(2,1)}, u32[]{:S(2)}, u32[]{:S(2)}) collective-permute-start(bf16[512,128]{1,0:T(8,128)(2,1)S(1)} %copy.52), channel_id=1, source_target_pairs={{0,1},{1,2},{2,3},{3,4},{4,5},{5,6},{6,7},{7,8},{8,9},{9,10},{10,1... | collective-permute-start | bytes 393224 | tf_op jit(solution)/shard_map/while/body/eval_jaxpr/ppermute | solution.py:43
  267.1 23.2 %collective-permute-start.1 = (bf16[512,128]{1,0:T(8,128)(2,1)}, bf16[512,128]{1,0:T(8,128)(2,1)}, u32[]{:S(2)}, u32[]{:S(2)}) collective-permute-start(bf16[512,128]{1,0:T(8,128)(2,1)} %copy.53), channel_id=1, source_target_pairs={{0,1},{1,2},{2,3},{3,4},{4,5},{5,6},{6,7},{7,8},{8,9},{9,10},{10,1... | collective-permute-start | bytes 393224 | tf_op jit(solution)/shard_map/while/body/eval_jaxpr/ppermute | solution.py:44
  292.8 20.4 %collective-permute-start.3 = (f32[512,128]{1,0:T(8,128)}, f32[512,128]{1,0:T(8,128)}, u32[]{:S(2)}, u32[]{:S(2)}) collective-permute-start(f32[512,128]{1,0:T(8,128)} %get-tuple-element.394), channel_id=1, source_target_pairs={{0,1},{1,2},{2,3},{3,4},{4,5},{5,6},{6,7},{7,8},{8,9},{9,10},{10,1... | collective-permute-start | bytes 786440 | tf_op jit(solution)/shard_map/while/body/eval_jaxpr/ppermute | solution.py:46
  292.8 22.1 %collective-permute-start = (bf16[512,128]{1,0:T(8,128)(2,1)S(1)}, bf16[512,128]{1,0:T(8,128)(2,1)}, u32[]{:S(2)}, u32[]{:S(2)}) collective-permute-start(bf16[512,128]{1,0:T(8,128)(2,1)S(1)} %copy.52), channel_id=1, source_target_pairs={{0,1},{1,2},{2,3},{3,4},{4,5},{5,6},{6,7},{7,8},{8,9},{9,10},{10,1... | collective-permute-start | bytes 393224 | tf_op jit(solution)/shard_map/while/body/eval_jaxpr/ppermute | solution.py:43
  292.9 23.2 %collective-permute-start.1 = (bf16[512,128]{1,0:T(8,128)(2,1)}, bf16[512,128]{1,0:T(8,128)(2,1)}, u32[]{:S(2)}, u32[]{:S(2)}) collective-permute-start(bf16[512,128]{1,0:T(8,128)(2,1)} %copy.53), channel_id=1, source_target_pairs={{0,1},{1,2},{2,3},{3,4},{4,5},{5,6},{6,7},{7,8},{8,9},{9,10},{10,1... | collective-permute-start | bytes 393224 | tf_op jit(solution)/shard_map/while/body/eval_jaxpr/ppermute | solution.py:44
  318.6 20.4 %collective-permute-start.3 = (f32[512,128]{1,0:T(8,128)}, f32[512,128]{1,0:T(8,128)}, u32[]{:S(2)}, u32[]{:S(2)}) collective-permute-start(f32[512,128]{1,0:T(8,128)} %get-tuple-element.394), channel_id=1, source_target_pairs={{0,1},{1,2},{2,3},{3,4},{4,5},{5,6},{6,7},{7,8},{8,9},{9,10},{10,1... | collective-permute-start | bytes 786440 | tf_op jit(solution)/shard_map/while/body/eval_jaxpr/ppermute | solution.py:46
  318.6 22.1 %collective-permute-start = (bf16[512,128]{1,0:T(8,128)(2,1)S(1)}, bf16[512,128]{1,0:T(8,128)(2,1)}, u32[]{:S(2)}, u32[]{:S(2)}) collective-permute-start(bf16[512,128]{1,0:T(8,128)(2,1)S(1)} %copy.52), channel_id=1, source_target_pairs={{0,1},{1,2},{2,3},{3,4},{4,5},{5,6},{6,7},{7,8},{8,9},{9,10},{10,1... | collective-permute-start | bytes 393224 | tf_op jit(solution)/shard_map/while/body/eval_jaxpr/ppermute | solution.py:43
  318.6 23.2 %collective-permute-start.1 = (bf16[512,128]{1,0:T(8,128)(2,1)}, bf16[512,128]{1,0:T(8,128)(2,1)}, u32[]{:S(2)}, u32[]{:S(2)}) collective-permute-start(bf16[512,128]{1,0:T(8,128)(2,1)} %copy.53), channel_id=1, source_target_pairs={{0,1},{1,2},{2,3},{3,4},{4,5},{5,6},{6,7},{7,8},{8,9},{9,10},{10,1... | collective-permute-start | bytes 393224 | tf_op jit(solution)/shard_map/while/body/eval_jaxpr/ppermute | solution.py:44
  344.3 20.4 %collective-permute-start.3 = (f32[512,128]{1,0:T(8,128)}, f32[512,128]{1,0:T(8,128)}, u32[]{:S(2)}, u32[]{:S(2)}) collective-permute-start(f32[512,128]{1,0:T(8,128)} %get-tuple-element.394), channel_id=1, source_target_pairs={{0,1},{1,2},{2,3},{3,4},{4,5},{5,6},{6,7},{7,8},{8,9},{9,10},{10,1... | collective-permute-start | bytes 786440 | tf_op jit(solution)/shard_map/while/body/eval_jaxpr/ppermute | solution.py:46
  344.3 22.1 %collective-permute-start = (bf16[512,128]{1,0:T(8,128)(2,1)S(1)}, bf16[512,128]{1,0:T(8,128)(2,1)}, u32[]{:S(2)}, u32[]{:S(2)}) collective-permute-start(bf16[512,128]{1,0:T(8,128)(2,1)S(1)} %copy.52), channel_id=1, source_target_pairs={{0,1},{1,2},{2,3},{3,4},{4,5},{5,6},{6,7},{7,8},{8,9},{9,10},{10,1... | collective-permute-start | bytes 393224 | tf_op jit(solution)/shard_map/while/body/eval_jaxpr/ppermute | solution.py:43
  344.3 23.2 %collective-permute-start.1 = (bf16[512,128]{1,0:T(8,128)(2,1)}, bf16[512,128]{1,0:T(8,128)(2,1)}, u32[]{:S(2)}, u32[]{:S(2)}) collective-permute-start(bf16[512,128]{1,0:T(8,128)(2,1)} %copy.53), channel_id=1, source_target_pairs={{0,1},{1,2},{2,3},{3,4},{4,5},{5,6},{6,7},{7,8},{8,9},{9,10},{10,1... | collective-permute-start | bytes 393224 | tf_op jit(solution)/shard_map/while/body/eval_jaxpr/ppermute | solution.py:44
  370.0 20.4 %collective-permute-start.3 = (f32[512,128]{1,0:T(8,128)}, f32[512,128]{1,0:T(8,128)}, u32[]{:S(2)}, u32[]{:S(2)}) collective-permute-start(f32[512,128]{1,0:T(8,128)} %get-tuple-element.394), channel_id=1, source_target_pairs={{0,1},{1,2},{2,3},{3,4},{4,5},{5,6},{6,7},{7,8},{8,9},{9,10},{10,1... | collective-permute-start | bytes 786440 | tf_op jit(solution)/shard_map/while/body/eval_jaxpr/ppermute | solution.py:46
  370.0 22.1 %collective-permute-start = (bf16[512,128]{1,0:T(8,128)(2,1)S(1)}, bf16[512,128]{1,0:T(8,128)(2,1)}, u32[]{:S(2)}, u32[]{:S(2)}) collective-permute-start(bf16[512,128]{1,0:T(8,128)(2,1)S(1)} %copy.52), channel_id=1, source_target_pairs={{0,1},{1,2},{2,3},{3,4},{4,5},{5,6},{6,7},{7,8},{8,9},{9,10},{10,1... | collective-permute-start | bytes 393224 | tf_op jit(solution)/shard_map/while/body/eval_jaxpr/ppermute | solution.py:43
  370.0 23.2 %collective-permute-start.1 = (bf16[512,128]{1,0:T(8,128)(2,1)}, bf16[512,128]{1,0:T(8,128)(2,1)}, u32[]{:S(2)}, u32[]{:S(2)}) collective-permute-start(bf16[512,128]{1,0:T(8,128)(2,1)} %copy.53), channel_id=1, source_target_pairs={{0,1},{1,2},{2,3},{3,4},{4,5},{5,6},{6,7},{7,8},{8,9},{9,10},{10,1... | collective-permute-start | bytes 393224 | tf_op jit(solution)/shard_map/while/body/eval_jaxpr/ppermute | solution.py:44
  395.6 18.3 %collective-permute-start.5 = (bf16[512,128]{1,0:T(8,128)(2,1)S(1)}, bf16[512,128]{1,0:T(8,128)(2,1)S(1)}, u32[]{:S(2)}, u32[]{:S(2)}) collective-permute-start(bf16[512,128]{1,0:T(8,128)(2,1)S(1)} %convert.12), channel_id=1, source_target_pairs={{0,1},{1,2},{2,3},{3,4},{4,5},{5,6},{6,7},{7,8},{8,9},{9,10},{10,1... | collective-permute-start | bytes 393224 | tf_op jit(solution)/shard_map/ppermute | solution.py:54
  395.7 21.1 %collective-permute-start.4 = (f32[512,128]{1,0:T(8,128)S(1)}, f32[512,128]{1,0:T(8,128)S(1)}, u32[]{:S(2)}, u32[]{:S(2)}) collective-permute-start(f32[512,128]{1,0:T(8,128)S(1)} %get-tuple-element.274), channel_id=1, source_target_pairs={{0,1},{1,2},{2,3},{3,4},{4,5},{5,6},{6,7},{7,8},{8,9},{9,10},{10,1... | collective-permute-start | bytes 786440 | tf_op jit(solution)/shard_map/ppermute | solution.py:53
  (34 other events, 468.6 us)
where the time goes:
time: 420 us; the launch traced here: 418 us
  waiting for transfers between devices  194 us (46%)
  starting transfers between devices  122 us (29%)
  local copies, waits for them, and re-layouts  84.7 us (20%)
  matrix products  11.6 us (3%)
  other arithmetic  5.03 us (1%)
    ppermute x15, waiting for transfers between devices, step_fn(): dk_next = lax.ppermute(dk_acc, 'cp', forward_perm)  131 us
    ppermute x15, starting transfers between devices, step_fn(): v_next = lax.ppermute(v_cur, 'cp', forward_perm)  54.7 us
    while x30, local copies, waits for them, and re-layouts  39.1 us
    another operation x30, local copies, waits for them, and re-layouts  37.1 us
    ppermute x15, starting transfers between devices, step_fn(): k_next = lax.ppermute(k_cur, 'cp', forward_perm)  32.3 us
    ppermute x15, starting transfers between devices, step_fn(): dv_next = lax.ppermute(dv_acc, 'cp', forward_perm)  27.6 us
    ppermute x15, waiting for transfers between devices, step_fn(): dv_next = lax.ppermute(dv_acc, 'cp', forward_perm)  25.7 us
    ppermute x15, waiting for transfers between devices, step_fn(): v_next = lax.ppermute(v_cur, 'cp', forward_perm)  17.3 us
  transfers between devices with their start and end apart: 62, of which 45 were waited for; matrix products, arithmetic and copies ran while one was open for 10% of the time, Pallas kernels for 0%

commit v1 on v0

v1 whole, which is shorter than its diff:
```python
import functools

import jax
import jax.numpy as jnp
from jax import lax
from jax.experimental import pallas as pl
from jax.experimental.pallas import tpu as pltpu
from jax.sharding import PartitionSpec as P

MESH = pl.DeviceIdType.MESH
LOG2E = 1.4426950408889634
F32, BF16 = jnp.float32, jnp.bfloat16
CHUNK = 512
UNIT = 4
GROUP = CHUNK * UNIT
UP, DOWN = 4, 3
OFFSETS = (0, 1, -2, -4, 3, -3, 2, -1)


def dot_nt(a, b):
    return lax.dot_general(a, b, (((1,), (1,)), ((), ())), preferred_element_type=F32)


def dot_tn(a, b):
    return lax.dot_general(a, b, (((0,), (0,)), ((), ())), preferred_element_type=F32)


def dot_nn(a, b):
    return jnp.dot(a, b, preferred_element_type=F32)


def kernel(n, scale, q_hbm, k_hbm, v_hbm, do_hbm, lse_hbm, dl_hbm, dq_out, dk_out, dv_out,
           q_all, do_all, lse_all, dl_all, kv_all, part, dq_all, dq_in, up_buf, dn_buf,
           load_sem, xs_sem, xr_sem, agu_s, agu_r, agd_s, agd_r, rsd_s, rsd_r, rsu_s, rsu_r, dqs_sem, dqr_sem):
    chips = n // 2
    me = lax.axis_index('cp')
    z = me // 2
    core = me % 2
    rows = q_hbm.shape[0]
    groups = rows // GROUP
    cols = k_hbm.shape[0]
    wrap = lambda i: lax.rem(i + 2 * chips, chips)
    above = {'cp': 2 * wrap(z + 1) + core}
    below = {'cp': 2 * wrap(z - 1) + core}
    sibling = {'cp': 2 * z + 1 - core}

    def need(chip, y):
        return wrap(y) < wrap(chip)

    def any_of(flags):
        return functools.reduce(jnp.logical_or, flags)

    def up_on(d, z0):
        return any_of([need(z0 + i, z0 - d) for i in range(UP - d + 1)])

    def dn_on(e, z0):
        return any_of([need(z0 - i, z0 + e) for i in range(DOWN - e + 1)])

    def remote(src, dst, ss, rs, to):
        return pltpu.make_async_remote_copy(src_ref=src, dst_ref=dst, send_sem=ss, recv_sem=rs, device_id=to, device_id_type=MESH)

    def ag_up(d):
        blk = kv_all.at[wrap(z - d + 1)]
        return remote(blk, blk, agu_s.at[d - 1], agu_r.at[d - 1], above)

    def ag_up_in(d):
        blk = kv_all.at[wrap(z - d)]
        return remote(blk, blk, agu_s.at[d - 1], agu_r.at[d - 1], above)

    def ag_dn(e):
        blk = kv_all.at[wrap(z + e - 1)]
        return remote(blk, blk, agd_s.at[e - 1], agd_r.at[e - 1], below)

    def ag_dn_in(e):
        blk = kv_all.at[wrap(z + e)]
        return remote(blk, blk, agd_s.at[e - 1], agd_r.at[e - 1], below)

    def rs_dn(d):
        return remote(part.at[wrap(z - d)], dn_buf.at[d - 1], rsd_s.at[d - 1], rsd_r.at[d - 1], below)

    def rs_up(e):
        return remote(part.at[wrap(z + e)], up_buf.at[e - 1], rsu_s.at[e - 1], rsu_r.at[e - 1], above)

    srcs = (q_hbm, do_hbm, lse_hbm, dl_hbm)
    dsts = (q_all, do_all, lse_all, dl_all)

    def swap(i, g):
        r = pl.ds(g * GROUP, GROUP)
        return remote(srcs[i].at[r], dsts[i].at[pl.ds(rows + g * GROUP, GROUP)], xs_sem.at[i, g], xr_sem.at[i, g], sibling)

    def load(i):
        return pltpu.make_async_copy(srcs[i], dsts[i].at[pl.ds(0, rows)], load_sem.at[i])

    def dq_swap():
        return remote(dq_all.at[pl.ds(rows, rows)], dq_in, dqs_sem, dqr_sem, sibling)

    load_k = pltpu.make_async_copy(k_hbm, kv_all.at[z, 0], load_sem.at[4])
    load_v = pltpu.make_async_copy(v_hbm, kv_all.at[z, 1], load_sem.at[5])
    load_k.start()
    load_v.start()
    for i in range(4):
        load(i).start()

    barrier = pltpu.get_barrier_semaphore()
    for peer in (above, below, sibling):
        pl.semaphore_signal(barrier, inc=1, device_id=peer, device_id_type=MESH)
    pl.semaphore_wait(barrier, 3)

    load_k.wait()
    load_v.wait()
    pl.when(up_on(1, z + 1))(lambda: ag_up(1).start())
    pl.when(dn_on(1, z - 1))(lambda: ag_dn(1).start())
    for g in range(groups):
        for i in range(4):
            swap(i, g).start()

    part[...] = jnp.zeros_like(part)
    dq_all[...] = jnp.zeros_like(dq_all)
    for i in range(4):
        load(i).wait()

    def tiles(y, base, units, mask_from):
        k = kv_all[y, 0]
        v = kv_all[y, 1]
        ps, dss = [], []
        for u in range(units):
            r = pl.ds(pl.multiple_of(base + u * CHUNK, CHUNK), CHUNK)
            s = dot_nt(q_all[r, :], k)
            dp = dot_nt(do_all[r, :], v)
            p = jnp.exp2(s * (scale * LOG2E) - jnp.tile(lse_all[r, :], (1, cols // 128)))
            if mask_from is not None:
                row = lax.broadcasted_iota(jnp.int32, p.shape, 0) + u * CHUNK
                col = lax.broadcasted_iota(jnp.int32, p.shape, 1) * 8 - mask_from
                p = jnp.where(col <= row, p, 0.0)
            dss.append((p * (dp - jnp.tile(dl_all[r, :], (1, cols // 128)))).astype(BF16))
            ps.append(p.astype(BF16))
        r = pl.ds(pl.multiple_of(base, CHUNK), CHUNK * units)
        ds = jnp.concatenate(dss, 0)
        part[y, 1] += dot_tn(do_all[r, :], jnp.concatenate(ps, 0))
        part[y, 0] += dot_tn(q_all[r, :], ds)
        dq_all[r, :] += dot_nn(ds, k)

    def diag(i, carry):
        base = i * (2 * CHUNK)
        tiles(z, base, 2, base)
        return carry

    lax.fori_loop(0, rows // (2 * CHUNK), diag, 0)

    def ag_step(d):
        @pl.when(up_on(d, z))
        def _():
            ag_up_in(d).wait_recv()
        if d < UP:
            pl.when(up_on(d + 1, z + 1))(lambda: ag_up(d + 1).start())
        if d <= DOWN:
            @pl.when(dn_on(d, z))
            def _():
                ag_dn_in(d).wait_recv()
        if d < DOWN:
            pl.when(dn_on(d + 1, z - 1))(lambda: ag_dn(d + 1).start())

    def rs_dn_step(d):
        if d < UP:
            @pl.when(up_on(d + 1, z + 1))
            def _():
                rs_dn(d + 1).wait_recv()
                part[wrap(z - d)] += dn_buf[d]
        pl.when(up_on(d, z))(lambda: rs_dn(d).start())

    def rs_up_step(e):
        if e < DOWN:
            @pl.when(dn_on(e + 1, z - 1))
            def _():
                rs_up(e + 1).wait_recv()
                part[wrap(z + e)] += up_buf[e]
        pl.when(dn_on(e, z))(lambda: rs_up(e).start())

    def swap_wait(g):
        for i in range(4):
            swap(i, g).wait_recv()

    hooks = {
        0: [lambda: swap_wait(0)],
        1: [lambda: swap_wait(1), lambda: ag_step(1)],
        5: [lambda: ag_step(2)],
        8: [lambda: ag_step(3)],
        12: [lambda: ag_step(4)],
        16: [lambda: rs_dn_step(4)],
        20: [lambda: rs_up_step(3)],
        24: [lambda: rs_dn_step(3)],
        27: [lambda: rs_dn_step(2)],
        28: [lambda: rs_up_step(2)],
        30: [lambda: dq_swap().start()],
        31: [lambda: rs_up_step(1)],
    }

    def sweep(t, carry):
        w = t // 4
        j = t % 4
        for at, fns in hooks.items():
            @pl.when(t == at)
            def _():
                for fn in fns:
                    fn()
        off = sum(jnp.where(w == i, o, 0) for i, o in enumerate(OFFSETS))
        y = wrap(z + off)
        mine = j // 2
        on = jnp.logical_or(jnp.logical_and(w > 0, need(z, y)), jnp.logical_and(w == 0, jnp.logical_and(mine == 0, core == 0)))

        @pl.when(on)
        def _():
            tiles(y, (1 - mine) * rows + (j % 2) * GROUP, UNIT, None)
        return carry

    lax.fori_loop(0, 4 * len(OFFSETS), sweep, 0)
    rs_dn_step(1)

    dq_swap().wait_recv()
    for g in range(rows // CHUNK):
        r = pl.ds(g * CHUNK, CHUNK)
        dq_out[r, :] = ((dq_all[r, :] + dq_in[r, :]) * scale).astype(BF16)

    @pl.when(up_on(1, z + 1))
    def _():
        rs_dn(1).wait_recv()
        part[z] += dn_buf[0]

    @pl.when(dn_on(1, z - 1))
    def _():
        rs_up(1).wait_recv()
        part[z] += up_buf[0]

    dk_out[...] = (part[z, 0] * scale).T.astype(BF16)
    dv_out[...] = part[z, 1].T.astype(BF16)

    for g in range(groups):
        for i in range(4):
            swap(i, g).wait_send()
    for d in range(1, UP + 1):
        pl.when(up_on(d, z + 1))(lambda d=d: ag_up(d).wait_send())
        pl.when(up_on(d, z))(lambda d=d: rs_dn(d).wait_send())
    for e in range(1, DOWN + 1):
        pl.when(dn_on(e, z - 1))(lambda e=e: ag_dn(e).wait_send())
        pl.when(dn_on(e, z))(lambda e=e: rs_up(e).wait_send())
    dq_swap().wait_send()


def solution(mesh):
    n = mesh.shape['cp']
    row_spec = P(('dp', 'cp'))

    def local_fn(q_tok, k_tok, v_tok, fwd_out, d_out, lse_row):
        toks, heads, dim = q_tok.shape
        rows = toks * heads
        scale = dim ** -0.5
        delta = jnp.einsum('rgd,rgd->rg', d_out, fwd_out, preferred_element_type=F32)
        wide = lambda x: jnp.broadcast_to(x[:, :, None], (toks, heads, 128)).reshape(rows, 128)
        flat = lambda x: x.reshape(rows, dim)
        chips = n // 2
        groups = rows // GROUP
        dma = pltpu.SemaphoreType.DMA
        dq, dk, dv = pl.pallas_call(
            functools.partial(kernel, n, scale),
            out_shape=(jax.ShapeDtypeStruct((rows, dim), BF16), jax.ShapeDtypeStruct((toks, dim), BF16), jax.ShapeDtypeStruct((toks, dim), BF16)),
            in_specs=[pl.BlockSpec(memory_space=pl.ANY)] * 6,
            out_specs=[pl.BlockSpec(memory_space=pltpu.VMEM)] * 3,
            scratch_shapes=[
                pltpu.VMEM((2 * rows, dim), BF16),
                pltpu.VMEM((2 * rows, dim), BF16),
                pltpu.VMEM((2 * rows, 128), F32),
                pltpu.VMEM((2 * rows, 128), F32),
                pltpu.VMEM((chips, 2, toks, dim), BF16),
                pltpu.VMEM((chips, 2, dim, toks), F32),
                pltpu.VMEM((2 * rows, dim), F32),
                pltpu.VMEM((rows, dim), F32),
                pltpu.VMEM((DOWN, 2, dim, toks), F32),
                pltpu.VMEM((UP, 2, dim, toks), F32),
                dma((6,)), dma((4, groups)), dma((4, groups)),
                dma((UP,)), dma((UP,)), dma((DOWN,)), dma((DOWN,)),
                dma((UP,)), dma((UP,)), dma((DOWN,)), dma((DOWN,)),
                dma, dma,
            ],
            compiler_params=pltpu.CompilerParams(collective_id=0, has_side_effects=True, vmem_limit_bytes=60 * 2 ** 20),
        )(flat(q_tok), k_tok, v_tok, flat(d_out), wide(lse_row * LOG2E), wide(delta))
        return dq.reshape(q_tok.shape), dk, dv

    return jax.shard_map(local_fn, mesh=mesh, in_specs=(row_spec,) * 6, out_specs=(row_spec,) * 3, check_vma=False)
```

time: 420 us -> 126 us (0.30)
  waiting for transfers between devices: 194 us -> 0 us
  starting transfers between devices: 122 us -> 0 us
  Pallas kernels: 0 us -> 114 us
  local copies, waits for them, and re-layouts: 84.7 us -> 7.91 us
  matrix products: 11.6 us -> 0 us
    ppermute x62 -> x0, waiting for transfers between devices: 194 us -> none  [the longest x15 131 us: step_fn(): dk_next = lax.ppermute(dk_acc, 'cp', forward_perm)]
    ppermute x62 -> x0, starting transfers between devices: 122 us -> none  [the longest x15 54.7 us: step_fn(): v_next = lax.ppermute(v_cur, 'cp', forward_perm)]
    pallas_call x0 -> x1, Pallas kernels: none -> 114 us  [local_fn(): pl.pallas_call(functools.partial(kernel, n, scale), out_shape=(jax.ShapeD...]
    while x32 -> x0, local copies, waits for them, and re-layouts: 41.5 us -> none
    another operation x30 -> x0, local copies, waits for them, and re-layouts: 37.1 us -> none
    dot_general x5 -> x0, matrix products: 11.6 us -> none  [the longest x1 4.62 us: pair_update(): jnp.einsum('rgc,rgd->cd', prob_low, d_out, preferred_element_type=jnp.flo...]
  transfers between devices with their start and end apart: 62 -> 0, of which waited for: 45 -> 0; matrix products, arithmetic and copies ran while one was open for 10% -> 0% of each run, Pallas kernels for 0% -> 0%
where the time goes in v1:
time: 126 us; the launch traced here: 125 us
  Pallas kernels  114 us (90%)
  local copies, waits for them, and re-layouts  7.91 us (6%)
  other arithmetic  2.89 us (2%)
    pallas_call x1, Pallas kernels, local_fn(): pl.pallas_call(functools.partial(kernel, n, scale), out_shape=(jax.ShapeD...  114 us
    broadcast_in_dim x4, local copies, waits for them, and re-layouts, local_fn(): jnp.broadcast_to(x[:, :, None], (toks, heads, 128)).reshape(rows, 128)  4.16 us
    unnamed x7, local copies, waits for them, and re-layouts  3.62 us

profile of v1, /device:TPU:30, one launch (start us, length us, event | category | flops | bytes accessed | tf_op | source)
XLA Modules:
  0.0 125.3 jit_solution(4378477782730980822)
XLA Ops:
  0.6 0.7 broadcast_multiply_fusion
  1.4 0.1 copy.9
  1.5 0.2 broadcast_in_dim.16
  1.6 2.2 %fusion = f32[512,8]{1,0:T(8,128)S(1)} fusion(bf16[512,8,128]{2,1,0:T(8,128)(2,1)} %param.10, bf16[512,8,128]{2,1,0:T(8,128)(2,1)} %param.9), kind=kLoop, calls=%fused_computation.1 | loop fusion | flops 2093056 | bytes 2113536 | tf_op jit(solution)/shard_map/rgd,rgd->rg/dot_general | solution.py:257
  3.8 0.1 broadcast_in_dim.18
  4.0 1.9 %broadcast_in_dim.19.dl_hbm = f32[4096,128]{1,0:T(8,128)} broadcast(f32[4096]{0:T(1024)S(1)} %broadcast_in_dim.18), dimensions={0} | broadcast | bytes 2113536 | tf_op jit(solution)/shard_map/broadcast_in_dim | solution.py:258
  5.9 2.0 %broadcast_in_dim.17.lse_hbm = f32[4096,128]{1,0:T(8,128)} broadcast(f32[4096]{0:T(1024)S(1)} %broadcast_in_dim.16), dimensions={0} | broadcast | bytes 2113536 | tf_op jit(solution)/shard_map/broadcast_in_dim | solution.py:258
  7.8 113.9 %shard_map.85 = (bf16[4096,128]{1,0:T(8,128)(2,1)}, bf16[512,128]{1,0:T(8,128)(2,1)}, bf16[512,128]{1,0:T(8,128)(2,1)}) custom-call(bf16[4096,128]{1,0:T(8,128)(2,1)} %bitcast.4, bf16[512,128]{1,0:T(8,128)(2,1)} %k_hbm.1, bf16[512,128]{1,0:T(8,128)(2,1)} %v_hbm.1, bf16[4096,128]{1,0:T(8,128)(2,1)} %bitcast.3, f32[4096,128]{1,0:T(8,128)} %broadcast_in_dim.17.lse_hbm, ...), custom_call_target="tpu_custom_call" | custom-call | tf_op jit(solution)/shard_map/pallas_call | solution.py:263
  121.7 0.0 copy-start.1
  121.7 0.0 copy-start
  121.7 2.3 %copy.18 = bf16[512,8,128]{2,1,0:T(8,128)(2,1)} copy(bf16[512,8,128]{2,1,0:T(8,128)(2,1)} %bitcast.5) | data formatting | bytes 2097152
  124.0 0.0 copy-done.1
  124.0 0.7 copy.19
  124.7 0.0 copy-done
  124.7 0.7 copy.20
Async XLA Ops:
  121.7 2.3 %copy-start.1 = (bf16[512,128]{1,0:T(8,128)(2,1)S(1)}, bf16[512,128]{1,0:T(8,128)(2,1)}, u32[]{:S(2)}) copy-start(bf16[512,128]{1,0:T(8,128)(2,1)} %get-tuple-element.13) | copy-start | bytes 393220
  121.7 3.0 %copy-start = (bf16[512,128]{1,0:T(8,128)(2,1)S(1)}, bf16[512,128]{1,0:T(8,128)(2,1)}, u32[]{:S(2)}) copy-start(bf16[512,128]{1,0:T(8,128)(2,1)} %get-tuple-element.14) | copy-start | bytes 393220

commit v2 on v1

v2 whole, which is shorter than its diff:
```python
import functools

import jax
import jax.numpy as jnp
from jax import lax
from jax.experimental import pallas as pl
from jax.experimental.pallas import tpu as pltpu
from jax.sharding import PartitionSpec as P

MESH = pl.DeviceIdType.MESH
LOG2E = 1.4426950408889634
F32, BF16 = jnp.float32, jnp.bfloat16
CHUNK = 512
UNIT = 4
GROUP = CHUNK * UNIT
UP, DOWN = (4, 3), (3, 4)
FAR = 4
OFFSETS = (1, -2, -4, -3, 3, 2, -1)


def dot_nt(a, b):
    return lax.dot_general(a, b, (((1,), (1,)), ((), ())), preferred_element_type=F32)


def dot_tn(a, b):
    return lax.dot_general(a, b, (((0,), (0,)), ((), ())), preferred_element_type=F32)


def dot_nn(a, b):
    return jnp.dot(a, b, preferred_element_type=F32)


def kernel(n, scale, q_hbm, k_hbm, v_hbm, out_hbm, do_hbm, lse_in, dq_out, dk_out, dv_out,
           q_all, do_all, fwd, lse_all, dl_all, stats, kv_all, part, dq_all, dq_in, up_buf, dn_buf,
           load_sem, xs_sem, xr_sem, agu_s, agu_r, agd_s, agd_r, rsd_s, rsd_r, rsu_s, rsu_r, dqs_sem, dqr_sem):
    chips = n // 2
    me = lax.axis_index('cp')
    z = me // 2
    core = me % 2
    rows = q_hbm.shape[0]
    halves = rows // GROUP
    cols, dim = k_hbm.shape
    heads = rows // cols
    wrap = lambda i: lax.rem(i + 2 * chips, chips)
    above = {'cp': 2 * wrap(z + 1) + core}
    below = {'cp': 2 * wrap(z - 1) + core}
    sibling = {'cp': 2 * z + 1 - core}

    def need(chip, y):
        return wrap(y) < wrap(chip)

    def any_of(flags):
        return functools.reduce(jnp.logical_or, flags)

    def up_on(d, z0, p):
        return any_of([need(z0 + i, z0 - d) for i in range(UP[p] - d + 1)])

    def dn_on(e, z0, p):
        return any_of([need(z0 - i, z0 + e) for i in range(DOWN[p] - e + 1)])

    def remote(src, dst, ss, rs, to):
        return pltpu.make_async_remote_copy(src_ref=src, dst_ref=dst, send_sem=ss, recv_sem=rs, device_id=to, device_id_type=MESH)

    def ag_up(d, p, dist):
        blk = kv_all.at[wrap(z - dist), p]
        return remote(blk, blk, agu_s.at[d - 1, p], agu_r.at[d - 1, p], above)

    def ag_dn(e, p, dist):
        blk = kv_all.at[wrap(z + dist), p]
        return remote(blk, blk, agd_s.at[e - 1, p], agd_r.at[e - 1, p], below)

    def rs_dn(d, p):
        return remote(part.at[wrap(z - d), p], dn_buf.at[d - 1, p], rsd_s.at[d - 1, p], rsd_r.at[d - 1, p], below)

    def rs_up(e, p):
        return remote(part.at[wrap(z + e), p], up_buf.at[e - 1, p], rsu_s.at[e - 1, p], rsu_r.at[e - 1, p], above)

    def swap(i, g):
        src, dst = ((q_hbm, q_all), (do_hbm, do_all))[i]
        return remote(src.at[pl.ds(g * GROUP, GROUP)], dst.at[pl.ds(rows + g * GROUP, GROUP)], xs_sem.at[i, g], xr_sem.at[i, g], sibling)

    def swap_stats():
        return remote(stats.at[0], stats.at[1], xs_sem.at[2, 0], xr_sem.at[2, 0], sibling)

    def dq_swap():
        return remote(dq_all.at[pl.ds(rows, rows)], dq_in, dqs_sem, dqr_sem, sibling)

    local = [
        pltpu.make_async_copy(k_hbm, kv_all.at[z, 0], load_sem.at[0]),
        pltpu.make_async_copy(v_hbm, kv_all.at[z, 1], load_sem.at[1]),
        pltpu.make_async_copy(do_hbm, do_all.at[pl.ds(0, rows)], load_sem.at[2]),
        pltpu.make_async_copy(out_hbm, fwd, load_sem.at[3]),
        pltpu.make_async_copy(q_hbm, q_all.at[pl.ds(0, rows)], load_sem.at[4]),
    ]
    for c in local:
        c.start()

    barrier = pltpu.get_barrier_semaphore()
    for peer in (above, below, sibling):
        pl.semaphore_signal(barrier, inc=1, device_id=peer, device_id_type=MESH)
    pl.semaphore_wait(barrier, 3)

    for p in range(2):
        local[p].wait()
        pl.when(up_on(1, z + 1, p))(lambda: ag_up(1, p, 0).start())
        pl.when(dn_on(1, z - 1, p))(lambda: ag_dn(1, p, 0).start())
    for g in range(halves):
        for i in range(2):
            swap(i, g).start()

    def widen(x, dst, base):
        for t in range(128):
            dst[pl.ds(pl.multiple_of(base + t * heads, heads), heads), :] = jnp.broadcast_to(x[:, t:t + 1], (heads, 128))

    local[2].wait()
    local[3].wait()
    stats[0, 0] = lse_in[...] * LOG2E
    lane = lax.broadcasted_iota(jnp.int32, (heads, 128), 1)

    def own_stats(i, carry):
        at = pl.ds(pl.multiple_of(i * 128, 128), 128)
        base = i * (128 * heads)
        r = pl.ds(pl.multiple_of(base, 128 * heads), 128 * heads)
        d = jnp.sum(do_all[r, :].astype(F32) * fwd[r, :].astype(F32), axis=-1, keepdims=True)
        wide = jnp.broadcast_to(d, (128 * heads, 128))
        dl_all[r, :] = wide
        dense = jnp.zeros((heads, 128), F32)
        for t in range(128):
            dense = jnp.where(lane == t, wide[t * heads:(t + 1) * heads], dense)
        stats[0, 1, :, at] = dense
        widen(stats[0, 0, :, at], lse_all, base)
        return carry

    lax.fori_loop(0, cols // 128, own_stats, 0)
    local[4].wait()
    part[...] = jnp.zeros_like(part)
    dq_all[...] = jnp.zeros_like(dq_all)
    swap_stats().start()

    def tiles(y, base, units, width, mask_from):
        k = kv_all[y, 0, :width]
        v = kv_all[y, 1, :width]
        ps, dss = [], []
        for u in range(units):
            r = pl.ds(pl.multiple_of(base + u * CHUNK, CHUNK), CHUNK)
            s = dot_nt(q_all[r, :], k)
            dp = dot_nt(do_all[r, :], v)
            p = jnp.exp2(s * (scale * LOG2E) - jnp.tile(lse_all[r, :], (1, width // 128)))
            if mask_from is not None:
                row = lax.broadcasted_iota(jnp.int32, p.shape, 0) + u * CHUNK
                col = lax.broadcasted_iota(jnp.int32, p.shape, 1) * heads - mask_from
                p = jnp.where(col <= row, p, 0.0)
            dss.append((p * (dp - jnp.tile(dl_all[r, :], (1, width // 128)))).astype(BF16))
            ps.append(p.astype(BF16))
        r = pl.ds(pl.multiple_of(base, CHUNK), CHUNK * units)
        ds = jnp.concatenate(dss, 0)
        part[y, 1, :, :width] += dot_tn(do_all[r, :], jnp.concatenate(ps, 0))
        part[y, 0, :, :width] += dot_tn(q_all[r, :], ds)
        dq_all[r, :] += dot_nn(ds, k)

    pairs = rows // (2 * CHUNK)

    def diag(width, i, carry):
        base = i * (2 * CHUNK)
        tiles(z, base, 2, width, base)
        return carry

    lax.fori_loop(0, pairs // 2, functools.partial(diag, cols // 2), 0)
    lax.fori_loop(pairs // 2, pairs, functools.partial(diag, cols), 0)

    swap_stats().wait_recv()

    def sibling_stats(i, carry):
        at = pl.ds(pl.multiple_of(i * 128, 128), 128)
        base = rows + i * (128 * heads)
        widen(stats[1, 0, :, at], lse_all, base)
        widen(stats[1, 1, :, at], dl_all, base)
        return carry

    lax.fori_loop(0, cols // 128, sibling_stats, 0)

    def ag_step(d):
        for p in range(2):
            if d <= UP[p]:
                pl.when(up_on(d, z, p))(lambda: ag_up(d, p, d).wait_recv())
            if d < UP[p]:
                pl.when(up_on(d + 1, z + 1, p))(lambda: ag_up(d + 1, p, d).start())
            if d <= DOWN[p]:
                pl.when(dn_on(d, z, p))(lambda: ag_dn(d, p, d).wait_recv())
            if d < DOWN[p]:
                pl.when(dn_on(d + 1, z - 1, p))(lambda: ag_dn(d + 1, p, d).start())

    def step(d, p, reach, is_on, step_out, buf, y, away, early):
        comes = is_on(d + 1, z + away, p) if d < reach else None
        if early:
            go = is_on(d, z, p)
            if comes is not None:
                go = jnp.logical_and(go, jnp.logical_not(comes))
            pl.when(go)(lambda: step_out(d, p).start())
        elif comes is not None:
            @pl.when(comes)
            def _():
                step_out(d + 1, p).wait_recv()
                part[y, p] += buf[d, p]
                step_out(d, p).start()

    def dn(d, p, early):
        step(d, p, UP[p], up_on, rs_dn, dn_buf, wrap(z - d), 1, early)

    def up(e, p, early):
        step(e, p, DOWN[p], dn_on, rs_up, up_buf, wrap(z + e), -1, early)

    def both(f, d, p):
        f(d, p, True)
        f(d, p, False)

    def swap_wait():
        for g in range(halves):
            for i in range(2):
                swap(i, g).wait_recv()

    hooks = {
        0: lambda: (swap_wait(), ag_step(1)),
        3: lambda: ag_step(2),
        4: lambda: (up(1, 0, True), up(1, 1, True)),
        6: lambda: ag_step(3),
        8: lambda: (ag_step(4), dn(2, 0, True), dn(2, 1, True)),
        12: lambda: (both(dn, 4, 0), both(up, 4, 1)),
        16: lambda: (both(dn, 3, 0), both(dn, 3, 1)),
        19: lambda: dn(2, 0, False),
        20: lambda: (both(up, 3, 1), both(up, 3, 0)),
        21: lambda: dn(2, 1, False),
        24: lambda: (both(up, 2, 1), up(2, 0, True)),
        26: lambda: up(2, 0, False),
        27: lambda: up(1, 1, False),
        28: lambda: (both(dn, 1, 0), both(dn, 1, 1)),
    }

    def sweep(t, carry):
        w = t // 4
        j = t % 4
        for at, fn in hooks.items():
            @pl.when(t == at)
            def _():
                fn()
        off = sum(jnp.where(w == i, o, 0) for i, o in enumerate(OFFSETS))
        y = wrap(z + off)
        last = w == len(OFFSETS)
        on = jnp.logical_or(jnp.logical_and(jnp.logical_not(last), need(z, y)), jnp.logical_and(last, core == 0))

        @pl.when(on)
        def _():
            tiles(y, (1 - j // 2) * rows + (j % 2) * GROUP, UNIT, cols, None)
        return carry

    lax.fori_loop(0, 4 * len(OFFSETS) + 2, sweep, 0)
    dq_swap().start()
    up(1, 0, False)

    dq_swap().wait_recv()
    for g in range(rows // CHUNK):
        r = pl.ds(g * CHUNK, CHUNK)
        dq_out[r, :] = ((dq_all[r, :] + dq_in[r, :]) * scale).astype(BF16)

    for p in range(2):
        @pl.when(up_on(1, z + 1, p))
        def _():
            rs_dn(1, p).wait_recv()
            part[z, p] += dn_buf[0, p]

        @pl.when(dn_on(1, z - 1, p))
        def _():
            rs_up(1, p).wait_recv()
            part[z, p] += up_buf[0, p]

    dk_out[...] = (part[z, 0] * scale).T.astype(BF16)
    dv_out[...] = part[z, 1].T.astype(BF16)

    for g in range(halves):
        for i in range(2):
            swap(i, g).wait_send()
    swap_stats().wait_send()
    for p in range(2):
        for d in range(1, UP[p] + 1):
            pl.when(up_on(d, z + 1, p))(lambda: ag_up(d, p, d - 1).wait_send())
            pl.when(up_on(d, z, p))(lambda: rs_dn(d, p).wait_send())
        for e in range(1, DOWN[p] + 1):
            pl.when(dn_on(e, z - 1, p))(lambda: ag_dn(e, p, e - 1).wait_send())
            pl.when(dn_on(e, z, p))(lambda: rs_up(e, p).wait_send())
    dq_swap().wait_send()


def deliver(dq, dk, dv, dq_out, dk_out, dv_out, a, b, c, sem_in, sem_out):
    pieces = 4
    step = dq.shape[0] // pieces
    moves = [(dk, b, dk_out), (dv, c, dv_out)] + [tuple(x.at[pl.ds(i * step, step)] for x in (dq, a, dq_out)) for i in range(pieces)]
    ins = [pltpu.make_async_copy(s, m, sem_in.at[i]) for i, (s, m, _) in enumerate(moves)]
    outs = [pltpu.make_async_copy(m, d, sem_out.at[i]) for i, (_, m, d) in enumerate(moves)]
    for x in ins:
        x.start()
    for x, o in zip(ins, outs):
        x.wait()
        o.start()
    for o in outs:
        o.wait()


def solution(mesh):
    n = mesh.shape['cp']
    row_spec = P(('dp', 'cp'))

    def local_fn(q_tok, k_tok, v_tok, fwd_out, d_out, lse_row):
        toks, heads, dim = q_tok.shape
        rows = toks * heads
        scale = dim ** -0.5
        flat = lambda x: x.reshape(rows, dim)
        chips = n // 2
        halves = rows // GROUP
        dma = pltpu.SemaphoreType.DMA
        hbm, vmem = pl.BlockSpec(memory_space=pl.ANY), pl.BlockSpec(memory_space=pltpu.VMEM)
        shapes = (jax.ShapeDtypeStruct((rows, dim), BF16), jax.ShapeDtypeStruct((toks, dim), BF16), jax.ShapeDtypeStruct((toks, dim), BF16))
        hops = dma((FAR, 2))
        grads = pl.pallas_call(
            functools.partial(kernel, n, scale),
            out_shape=shapes,
            in_specs=[hbm] * 5 + [vmem],
            out_specs=[vmem] * 3,
            scratch_shapes=[
                pltpu.VMEM((2 * rows, dim), BF16),
                pltpu.VMEM((2 * rows, dim), BF16),
                pltpu.VMEM((rows, dim), BF16),
                pltpu.VMEM((2 * rows, 128), F32),
                pltpu.VMEM((2 * rows, 128), F32),
                pltpu.VMEM((2, 2, heads, toks), F32),
                pltpu.VMEM((chips, 2, toks, dim), BF16),
                pltpu.VMEM((chips, 2, dim, toks), F32),
                pltpu.VMEM((2 * rows, dim), F32),
                pltpu.VMEM((rows, dim), F32),
                pltpu.VMEM((FAR, 2, dim, toks), F32),
                pltpu.VMEM((FAR, 2, dim, toks), F32),
                dma((5,)), dma((3, halves)), dma((3, halves)),
                hops, hops, hops, hops, hops, hops, hops, hops,
                dma, dma,
            ],
            compiler_params=pltpu.CompilerParams(collective_id=0, has_side_effects=True, vmem_limit_bytes=60 * 2 ** 20),
        )(flat(q_tok), k_tok, v_tok, flat(fwd_out), flat(d_out), lse_row.T)
        dq, dk, dv = pl.pallas_call(
            deliver,
            out_shape=shapes,
            in_specs=[hbm] * 3,
            out_specs=[hbm] * 3,
            scratch_shapes=[pltpu.VMEM(s.shape, s.dtype) for s in shapes] + [dma((6,)), dma((6,))],
        )(*grads)
        return dq.reshape(q_tok.shape), dk, dv

    return jax.shard_map(local_fn, mesh=mesh, in_specs=(row_spec,) * 6, out_specs=(row_spec,) * 3, check_vma=False)
```

time: 126 us -> 109 us (0.87)
  local copies, waits for them, and re-layouts: 7.91 us -> 0 us
  Pallas kernels: 114 us -> 108 us
  other arithmetic: 2.89 us -> 0 us
    pallas_call x1 -> x2, Pallas kernels: 114 us -> 108 us  [the longest x1 106 us: local_fn(): pl.pallas_call(functools.partial(kernel, n, scale), out_shape=shapes, in_...]
    broadcast_in_dim x4 -> x0, local copies, waits for them, and re-layouts: 4.16 us -> none  [local_fn(): jnp.broadcast_to(x[:, :, None], (toks, heads, 128)).reshape(rows, 128)]
    unnamed x7 -> x0, local copies, waits for them, and re-layouts: 3.62 us -> none
    dot_general x1 -> x0, other arithmetic: 2.17 us -> none  [local_fn(): jnp.einsum('rgd,rgd->rg', d_out, fwd_out, preferred_element_type=F32)]
where the time goes in v2:
time: 109 us
  Pallas kernels  108 us (99%)
    pallas_call x1, Pallas kernels, local_fn(): pl.pallas_call(functools.partial(kernel, n, scale), out_shape=shapes, in_...  106 us

profile of v2, /device:TPU:30, one launch (start us, length us, event | category | flops | bytes accessed | tf_op | source)
XLA Modules:
  0.0 109.1 jit_solution(14095163779969608540)
XLA Ops:
  0.6 106.3 %shard_map.85 = (bf16[4096,128]{1,0:T(8,128)(2,1)}, bf16[512,128]{1,0:T(8,128)(2,1)}, bf16[512,128]{1,0:T(8,128)(2,1)}) custom-call(bf16[4096,128]{1,0:T(8,128)(2,1)} %bitcast.5, bf16[512,128]{1,0:T(8,128)(2,1)} %k_hbm.1, bf16[512,128]{1,0:T(8,128)(2,1)} %v_hbm.1, bf16[4096,128]{1,0:T(8,128)(2,1)} %bitcast.6, bf16[4096,128]{1,0:T(8,128)(2,1)} %bitcast.7, ...), custom_call_target="tpu_custom_call" | custom-call | tf_op jit(solution)/shard_map/pallas_call | solution.py:323
  106.9 2.1 %shard_map.86 = (bf16[4096,128]{1,0:T(8,128)(2,1)}, bf16[512,128]{1,0:T(8,128)(2,1)}, bf16[512,128]{1,0:T(8,128)(2,1)}) custom-call(bf16[4096,128]{1,0:T(8,128)(2,1)} %get-tuple-element.9.dq, bf16[512,128]{1,0:T(8,128)(2,1)} %get-tuple-element.10.dk, bf16[512,128]{1,0:T(8,128)(2,1)} %get-tuple-element.11.dv), custom_call_target="tpu_custom_call" | custom-call | tf_op jit(solution)/shard_map/pallas_call | solution.py:347

commit v3 on v2

--- a/solution.py
+++ b/solution.py
@@ -15,7 +15,27 @@
 GROUP = CHUNK * UNIT
 UP, DOWN = (4, 3), (3, 4)
 FAR = 4
-OFFSETS = (1, -2, -4, -3, 3, 2, -1)
+OFFSETS = (-2, -3, -4, 3, 2, 1, -1)
+SCHEDULE = {
+    -2: (('ag', 1, 0),),
+    -1: (('ag', 1, 1),),
+    0: (('ag', 2, 0), ('ag', 2, 1),),
+    4: (('ag', 3, 0), ('ag', 3, 1),),
+    7: (('ag', 4, 0),),
+    8: (('ag', 4, 1), ('dn', 3, 0, True), ('dn', 3, 1, True),),
+    12: (('dn', 4, 0, True), ('up', 4, 1, True),),
+    14: (('dn', 2, 0, True), ('dn', 2, 1, False),),
+    16: (('up', 3, 1, False), ('dn', 3, 0, False), ('up', 3, 0, True), ('dn', 2, 0, False),),
+    19: (('dn', 2, 1, True),),
+    21: (('up', 2, 1, False),),
+    23: (('up', 2, 0, False),),
+    27: (('up', 1, 1, False),),
+    28: (('dn', 1, 0, False),),
+    29: (('up', 3, 1, True), ('up', 1, 0, True),),
+    30: (('up', 1, 0, False), ('up', 1, 1, True),),
+    32: (('dn', 1, 0, True), ('dn', 1, 1, False), ('dn', 1, 1, True),),
+    34: (('up', 2, 0, True), ('up', 2, 1, True),),
+}
 
 
 def dot_nt(a, b):
@@ -31,8 +51,8 @@
 
 
 def kernel(n, scale, q_hbm, k_hbm, v_hbm, out_hbm, do_hbm, lse_in, dq_out, dk_out, dv_out,
-           q_all, do_all, fwd, lse_all, dl_all, stats, kv_all, part, dq_all, dq_in, up_buf, dn_buf,
-           load_sem, xs_sem, xr_sem, agu_s, agu_r, agd_s, agd_r, rsd_s, rsd_r, rsu_s, rsu_r, dqs_sem, dqr_sem):
+           q_all, do_all, fwd, lse_all, dl_all, stats, kv_all, part, cross, dq_all, dq_in, up_buf, dn_buf,
+           load_sem, xs_sem, xr_sem, agu_s, agu_r, agd_s, agd_r, rsd_s, rsd_r, rsu_s, rsu_r, dqs_sem, dqr_sem, cs_sem, cr_sem, home_s, home_r):
     chips = n // 2
     me = lax.axis_index('cp')
     z = me // 2
@@ -72,6 +92,22 @@
     def rs_dn(d, p):
         return remote(part.at[wrap(z - d), p], dn_buf.at[d - 1, p], rsd_s.at[d - 1, p], rsd_r.at[d - 1, p], below)
 
+    def rs_home(p, h):
+        at = pl.ds(h * (cols // 2), cols // 2)
+        return remote(part.at[wrap(z - 1), p, :, at], dn_buf.at[0, p, :, at], home_s.at[p, h], home_r.at[p, h], below)
+
+    def home(h, early):
+        comes = up_on(2, z + 1, 0)
+        go = jnp.logical_and(up_on(1, z, 0), jnp.logical_not(comes)) if early else comes
+
+        @pl.when(go)
+        def _():
+            for p in range(2):
+                if not early and h == 0:
+                    rs_dn(2, p).wait_recv()
+                    part[wrap(z - 1), p] += dn_buf[1, p]
+                rs_home(p, h).start()
+
     def rs_up(e, p):
         return remote(part.at[wrap(z + e), p], up_buf.at[e - 1, p], rsu_s.at[e - 1, p], rsu_r.at[e - 1, p], above)
 
@@ -82,8 +118,54 @@
     def swap_stats():
         return remote(stats.at[0], stats.at[1], xs_sem.at[2, 0], xr_sem.at[2, 0], sibling)
 
+    def cross_kv(p):
+        return remote((k_hbm, v_hbm)[p], kv_all.at[chips, p], cs_sem.at[p], cr_sem.at[p], sibling)
+
+    def cross_sum():
+        return remote(part.at[chips], cross, cs_sem.at[2], cr_sem.at[2], sibling)
+
     def dq_swap():
         return remote(dq_all.at[pl.ds(rows, rows)], dq_in, dqs_sem, dqr_sem, sibling)
+
+    def ag_step(d, p):
+        if d <= UP[p]:
+            pl.when(up_on(d, z, p))(lambda: ag_up(d, p, d).wait_recv())
+        if d < UP[p]:
+            pl.when(up_on(d + 1, z + 1, p))(lambda: ag_up(d + 1, p, d).start())
+        if d <= DOWN[p]:
+            pl.when(dn_on(d, z, p))(lambda: ag_dn(d, p, d).wait_recv())
+        if d < DOWN[p]:
+            pl.when(dn_on(d + 1, z - 1, p))(lambda: ag_dn(d + 1, p, d).start())
+
+    def step(d, p, reach, is_on, step_out, buf, y, away, early):
+        comes = is_on(d + 1, z + away, p) if d < reach else None
+        if early:
+            go = is_on(d, z, p)
+            if comes is not None:
+                go = jnp.logical_and(go, jnp.logical_not(comes))
+            pl.when(go)(lambda: step_out(d, p).start())
+        elif comes is not None:
+            @pl.when(comes)
+            def _():
+                step_out(d + 1, p).wait_recv()
+                part[y, p] += buf[d, p]
+                step_out(d, p).start()
+
+    def dn(d, p, early):
+        if d == 1:
+            if not early:
+                home(p, False)
+            return
+        step(d, p, UP[p], up_on, rs_dn, dn_buf, wrap(z - d), 1, early)
+
+    def up(e, p, early):
+        step(e, p, DOWN[p], dn_on, rs_up, up_buf, wrap(z + e), -1, early)
+
+    moves = {'ag': ag_step, 'dn': dn, 'up': up}
+
+    def late(t):
+        for name, *args in SCHEDULE.get(t, ()):
+            moves[name](*args)
 
     local = [
         pltpu.make_async_copy(k_hbm, kv_all.at[z, 0], load_sem.at[0]),
@@ -107,6 +189,11 @@
     for g in range(halves):
         for i in range(2):
             swap(i, g).start()
+
+    @pl.when(core == 0)
+    def _():
+        for p in range(2):
+            cross_kv(p).start()
 
     def widen(x, dst, base):
         for t in range(128):
@@ -137,9 +224,10 @@
     dq_all[...] = jnp.zeros_like(dq_all)
     swap_stats().start()
 
-    def tiles(y, base, units, width, mask_from):
-        k = kv_all[y, 0, :width]
-        v = kv_all[y, 1, :width]
+    def tiles(y, base, units, width, mask_from, c0=0):
+        at = pl.ds(c0, width)
+        k = kv_all[y, 0, at]
+        v = kv_all[y, 1, at]
         ps, dss = [], []
         for u in range(units):
             r = pl.ds(pl.multiple_of(base + u * CHUNK, CHUNK), CHUNK)
@@ -154,8 +242,8 @@
             ps.append(p.astype(BF16))
         r = pl.ds(pl.multiple_of(base, CHUNK), CHUNK * units)
         ds = jnp.concatenate(dss, 0)
-        part[y, 1, :, :width] += dot_tn(do_all[r, :], jnp.concatenate(ps, 0))
-        part[y, 0, :, :width] += dot_tn(q_all[r, :], ds)
+        part[y, 1, :, at] += dot_tn(do_all[r, :], jnp.concatenate(ps, 0))
+        part[y, 0, :, at] += dot_tn(q_all[r, :], ds)
         dq_all[r, :] += dot_nn(ds, k)
 
     pairs = rows // (2 * CHUNK)
@@ -165,9 +253,9 @@
         tiles(z, base, 2, width, base)
         return carry
 
+    late(-2)
     lax.fori_loop(0, pairs // 2, functools.partial(diag, cols // 2), 0)
-    lax.fori_loop(pairs // 2, pairs, functools.partial(diag, cols), 0)
-
+    late(-1)
     swap_stats().wait_recv()
 
     def sibling_stats(i, carry):
@@ -179,93 +267,75 @@
 
     lax.fori_loop(0, cols // 128, sibling_stats, 0)
 
-    def ag_step(d):
-        for p in range(2):
-            if d <= UP[p]:
-                pl.when(up_on(d, z, p))(lambda: ag_up(d, p, d).wait_recv())
-            if d < UP[p]:
-                pl.when(up_on(d + 1, z + 1, p))(lambda: ag_up(d + 1, p, d).start())
-            if d <= DOWN[p]:
-                pl.when(dn_on(d, z, p))(lambda: ag_dn(d, p, d).wait_recv())
-            if d < DOWN[p]:
-                pl.when(dn_on(d + 1, z - 1, p))(lambda: ag_dn(d + 1, p, d).start())
-
-    def step(d, p, reach, is_on, step_out, buf, y, away, early):
-        comes = is_on(d + 1, z + away, p) if d < reach else None
-        if early:
-            go = is_on(d, z, p)
-            if comes is not None:
-                go = jnp.logical_and(go, jnp.logical_not(comes))
-            pl.when(go)(lambda: step_out(d, p).start())
-        elif comes is not None:
-            @pl.when(comes)
-            def _():
-                step_out(d + 1, p).wait_recv()
-                part[y, p] += buf[d, p]
-                step_out(d, p).start()
-
-    def dn(d, p, early):
-        step(d, p, UP[p], up_on, rs_dn, dn_buf, wrap(z - d), 1, early)
-
-    def up(e, p, early):
-        step(e, p, DOWN[p], dn_on, rs_up, up_buf, wrap(z + e), -1, early)
-
-    def both(f, d, p):
-        f(d, p, True)
-        f(d, p, False)
-
     def swap_wait():
         for g in range(halves):
             for i in range(2):
                 swap(i, g).wait_recv()
 
-    hooks = {
-        0: lambda: (swap_wait(), ag_step(1)),
-        3: lambda: ag_step(2),
-        4: lambda: (up(1, 0, True), up(1, 1, True)),
-        6: lambda: ag_step(3),
-        8: lambda: (ag_step(4), dn(2, 0, True), dn(2, 1, True)),
-        12: lambda: (both(dn, 4, 0), both(up, 4, 1)),
-        16: lambda: (both(dn, 3, 0), both(dn, 3, 1)),
-        19: lambda: dn(2, 0, False),
-        20: lambda: (both(up, 3, 1), both(up, 3, 0)),
-        21: lambda: dn(2, 1, False),
-        24: lambda: (both(up, 2, 1), up(2, 0, True)),
-        26: lambda: up(2, 0, False),
-        27: lambda: up(1, 1, False),
-        28: lambda: (both(dn, 1, 0), both(dn, 1, 1)),
-    }
+    full = 4 * (len(OFFSETS) - 1)
+    end = full + 8
+
+    def rows_of(j):
+        return (1 - j // 2) * rows + (j % 2) * GROUP
 
     def sweep(t, carry):
-        w = t // 4
-        j = t % 4
-        for at, fn in hooks.items():
-            @pl.when(t == at)
-            def _():
-                fn()
-        off = sum(jnp.where(w == i, o, 0) for i, o in enumerate(OFFSETS))
+        for at in SCHEDULE:
+            if 0 <= at < full:
+                pl.when(t == at)(lambda: late(at))
+        off = sum(jnp.where(t // 4 == i, o, 0) for i, o in enumerate(OFFSETS[:-1]))
         y = wrap(z + off)
-        last = w == len(OFFSETS)
-        on = jnp.logical_or(jnp.logical_and(jnp.logical_not(last), need(z, y)), jnp.logical_and(last, core == 0))
-
-        @pl.when(on)
+
+        @pl.when(need(z, y))
         def _():
-            tiles(y, (1 - j // 2) * rows + (j % 2) * GROUP, UNIT, cols, None)
+            tiles(y, rows_of(t % 4), UNIT, cols, None)
         return carry
 
-    lax.fori_loop(0, 4 * len(OFFSETS) + 2, sweep, 0)
+    def sweep_half(h, t, carry):
+        for at in SCHEDULE:
+            if full + 4 * h <= at < full + 4 * h + 4:
+                pl.when(t == at)(lambda: late(at))
+        y = wrap(z + OFFSETS[-1])
+
+        @pl.when(need(z, y))
+        def _():
+            tiles(y, rows_of(t % 4), UNIT, cols // 2, None, h * (cols // 2))
+        return carry
+
+    swap_wait()
+    lax.fori_loop(0, full, sweep, 0)
+    for h in range(2):
+        lax.fori_loop(full + 4 * h, full + 4 * h + 4, functools.partial(sweep_half, h), 0)
+        home(h, True)
+    late(end)
+
+    @pl.when(core == 1)
+    def _():
+        for p in range(2):
+            cross_kv(p).wait_recv()
+
+    crossed = jnp.where(core == 0, z, chips)
+    tiles(crossed, rows_of(jnp.where(core == 0, 0, 3)), UNIT, cols, None)
     dq_swap().start()
-    up(1, 0, False)
+    pl.when(core == 1)(lambda: cross_sum().start())
+    late(end + 1)
+    lax.fori_loop(pairs // 2, pairs, functools.partial(diag, cols), 0)
+    late(end + 2)
 
     dq_swap().wait_recv()
     for g in range(rows // CHUNK):
         r = pl.ds(g * CHUNK, CHUNK)
         dq_out[r, :] = ((dq_all[r, :] + dq_in[r, :]) * scale).astype(BF16)
 
+    @pl.when(core == 0)
+    def _():
+        cross_sum().wait_recv()
+        part[z] += cross[...]
+
     for p in range(2):
         @pl.when(up_on(1, z + 1, p))
         def _():
-            rs_dn(1, p).wait_recv()
+            for h in range(2):
+                rs_home(p, h).wait_recv()
             part[z, p] += dn_buf[0, p]
 
         @pl.when(dn_on(1, z - 1, p))
@@ -280,10 +350,20 @@
         for i in range(2):
             swap(i, g).wait_send()
     swap_stats().wait_send()
+
+    @pl.when(core == 0)
+    def _():
+        for p in range(2):
+            cross_kv(p).wait_send()
+
+    pl.when(core == 1)(lambda: cross_sum().wait_send())
     for p in range(2):
         for d in range(1, UP[p] + 1):
             pl.when(up_on(d, z + 1, p))(lambda: ag_up(d, p, d - 1).wait_send())
-            pl.when(up_on(d, z, p))(lambda: rs_dn(d, p).wait_send())
+            if d > 1:
+                pl.when(up_on(d, z, p))(lambda: rs_dn(d, p).wait_send())
+        for h in range(2):
+            pl.when(up_on(1, z, p))(lambda: rs_home(p, h).wait_send())
         for e in range(1, DOWN[p] + 1):
             pl.when(dn_on(e, z - 1, p))(lambda: ag_dn(e, p, e - 1).wait_send())
             pl.when(dn_on(e, z, p))(lambda: rs_up(e, p).wait_send())
@@ -332,15 +412,16 @@
                 pltpu.VMEM((2 * rows, 128), F32),
                 pltpu.VMEM((2 * rows, 128), F32),
                 pltpu.VMEM((2, 2, heads, toks), F32),
-                pltpu.VMEM((chips, 2, toks, dim), BF16),
-                pltpu.VMEM((chips, 2, dim, toks), F32),
+                pltpu.VMEM((chips + 1, 2, toks, dim), BF16),
+                pltpu.VMEM((chips + 1, 2, dim, toks), F32),
+                pltpu.VMEM((2, dim, toks), F32),
                 pltpu.VMEM((2 * rows, dim), F32),
                 pltpu.VMEM((rows, dim), F32),
                 pltpu.VMEM((FAR, 2, dim, toks), F32),
                 pltpu.VMEM((FAR, 2, dim, toks), F32),
                 dma((5,)), dma((3, halves)), dma((3, halves)),
                 hops, hops, hops, hops, hops, hops, hops, hops,
-                dma, dma,
+                dma, dma, dma((3,)), dma((3,)), dma((2, 2)), dma((2, 2)),
             ],
             compiler_params=pltpu.CompilerParams(collective_id=0, has_side_effects=True, vmem_limit_bytes=60 * 2 ** 20),
         )(flat(q_tok), k_tok, v_tok, flat(fwd_out), flat(d_out), lse_row.T)

time: 109 us -> 103 us (0.945)
  Pallas kernels: 108 us -> 102 us
    pallas_call x1, Pallas kernels: 106 us -> 100 us  [local_fn(): pl.pallas_call(functools.partial(kernel, n, scale), out_shape=shapes, in_...]
where the time goes in v3:
time: 103 us
  Pallas kernels  102 us (99%)
    pallas_call x1, Pallas kernels, local_fn(): pl.pallas_call(functools.partial(kernel, n, scale), out_shape=shapes, in_...  100 us
    pallas_call x1, Pallas kernels, local_fn(): pl.pallas_call(deliver, out_shape=shapes, in_specs=[hbm] * 3, out_specs=[...  2.15 us

profile of v3, /device:TPU:30, one launch (start us, length us, event | category | flops | bytes accessed | tf_op | source)
XLA Modules:
  0.0 102.9 jit_solution(16777401939541156126)
XLA Ops:
  0.6 100.0 %shard_map.85 = (bf16[4096,128]{1,0:T(8,128)(2,1)}, bf16[512,128]{1,0:T(8,128)(2,1)}, bf16[512,128]{1,0:T(8,128)(2,1)}) custom-call(bf16[4096,128]{1,0:T(8,128)(2,1)} %bitcast.5, bf16[512,128]{1,0:T(8,128)(2,1)} %k_hbm.1, bf16[512,128]{1,0:T(8,128)(2,1)} %v_hbm.1, bf16[4096,128]{1,0:T(8,128)(2,1)} %bitcast.6, bf16[4096,128]{1,0:T(8,128)(2,1)} %bitcast.7, ...), custom_call_target="tpu_custom_call" | custom-call | tf_op jit(solution)/shard_map/pallas_call | solution.py:403
  100.6 2.1 %shard_map.86 = (bf16[4096,128]{1,0:T(8,128)(2,1)}, bf16[512,128]{1,0:T(8,128)(2,1)}, bf16[512,128]{1,0:T(8,128)(2,1)}) custom-call(bf16[4096,128]{1,0:T(8,128)(2,1)} %get-tuple-element.9.dq, bf16[512,128]{1,0:T(8,128)(2,1)} %get-tuple-element.10.dk, bf16[512,128]{1,0:T(8,128)(2,1)} %get-tuple-element.11.dv), custom_call_target="tpu_custom_call" | custom-call | tf_op jit(solution)/shard_map/pallas_call | solution.py:428

commit v4 on v3

--- a/solution.py
+++ b/solution.py
@@ -8,6 +8,8 @@
 from jax.sharding import PartitionSpec as P
 
 MESH = pl.DeviceIdType.MESH
+HELP_AT = 10
+LENT = 3
 LOG2E = 1.4426950408889634
 F32, BF16 = jnp.float32, jnp.bfloat16
 CHUNK = 512
@@ -15,26 +17,30 @@
 GROUP = CHUNK * UNIT
 UP, DOWN = (4, 3), (3, 4)
 FAR = 4
-OFFSETS = (-2, -3, -4, 3, 2, 1, -1)
+OFFSETS = (-2, -3, -4, 3, 1, 2, -1)
 SCHEDULE = {
     -2: (('ag', 1, 0),),
     -1: (('ag', 1, 1),),
     0: (('ag', 2, 0), ('ag', 2, 1),),
     4: (('ag', 3, 0), ('ag', 3, 1),),
+    6: (('dn', 2, 0, True),),
     7: (('ag', 4, 0),),
-    8: (('ag', 4, 1), ('dn', 3, 0, True), ('dn', 3, 1, True),),
-    12: (('dn', 4, 0, True), ('up', 4, 1, True),),
-    14: (('dn', 2, 0, True), ('dn', 2, 1, False),),
-    16: (('up', 3, 1, False), ('dn', 3, 0, False), ('up', 3, 0, True), ('dn', 2, 0, False),),
-    19: (('dn', 2, 1, True),),
-    21: (('up', 2, 1, False),),
-    23: (('up', 2, 0, False),),
-    27: (('up', 1, 1, False),),
-    28: (('dn', 1, 0, False),),
-    29: (('up', 3, 1, True), ('up', 1, 0, True),),
-    30: (('up', 1, 0, False), ('up', 1, 1, True),),
-    32: (('dn', 1, 0, True), ('dn', 1, 1, False), ('dn', 1, 1, True),),
-    34: (('up', 2, 0, True), ('up', 2, 1, True),),
+    8: (('ag', 4, 1),),
+    9: (('dn', 3, 1, True),),
+    12: (('up', 4, 1, True), ('dn', 4, 0, True),),
+    14: (('dn', 3, 0, True), ('dn', 2, 1, False),),
+    16: (('up', 3, 0, True),),
+    17: (('dn', 3, 0, False),),
+    18: (('up', 3, 1, False),),
+    23: (('dn', 2, 0, False),),
+    24: (('dn', 2, 1, True), ('up', 2, 0, False),),
+    25: (('up', 3, 1, True),),
+    27: (('up', 1, 0, True),),
+    28: (('up', 2, 1, False),),
+    29: (('dn', 1, 0, False), ('up', 2, 1, True),),
+    32: (('up', 1, 0, False), ('dn', 1, 1, False), ('dn', 1, 0, True), ('dn', 1, 1, True),),
+    33: (('up', 2, 0, True), ('up', 1, 1, False),),
+    34: (('up', 1, 1, True),),
 }
 
 
@@ -51,8 +57,8 @@
 
 
 def kernel(n, scale, q_hbm, k_hbm, v_hbm, out_hbm, do_hbm, lse_in, dq_out, dk_out, dv_out,
-           q_all, do_all, fwd, lse_all, dl_all, stats, kv_all, part, cross, dq_all, dq_in, up_buf, dn_buf,
-           load_sem, xs_sem, xr_sem, agu_s, agu_r, agd_s, agd_r, rsd_s, rsd_r, rsu_s, rsu_r, dqs_sem, dqr_sem, cs_sem, cr_sem, home_s, home_r):
+           q_all, do_all, fwd, lse_all, dl_all, stats, kv_all, part, cross, dq_all, lent_dq, dq_in, up_buf, dn_buf,
+           load_sem, xs_sem, xr_sem, agu_s, agu_r, agd_s, agd_r, rsd_s, rsd_r, rsu_s, rsu_r, dqs_sem, dqr_sem, cs_sem, cr_sem, home_s, home_r, lend_s, lend_r, pass_s, pass_r, back_s, back_r):
     chips = n // 2
     me = lax.axis_index('cp')
     z = me // 2
@@ -123,6 +129,27 @@
 
     def cross_sum():
         return remote(part.at[chips], cross, cs_sem.at[2], cr_sem.at[2], sibling)
+
+    lender, helper = z == chips - 1, z == 0
+    theirs = pl.ds(2 * rows, GROUP)
+    theirs_too = pl.ds(2 * rows + GROUP, GROUP)
+
+    def lend(i):
+        half = pl.ds(rows - GROUP, GROUP)
+        src = (q_hbm.at[half], do_hbm.at[half], stats.at[0])[i]
+        dst = (q_all.at[theirs], do_all.at[theirs], stats.at[2])[i]
+        return remote(src, dst, lend_s.at[i], lend_r.at[i], above)
+
+    def pass_on(i):
+        src = (q_all.at[theirs], do_all.at[theirs], stats.at[2])[i]
+        dst = (q_all.at[theirs_too], do_all.at[theirs_too], stats.at[3])[i]
+        return remote(src, dst, pass_s.at[i], pass_r.at[i], sibling)
+
+    def merge():
+        return remote(dq_all.at[theirs_too], lent_dq, back_s.at[0], back_r.at[0], sibling)
+
+    def give_back():
+        return remote(dq_all.at[theirs], lent_dq, back_s.at[1], back_r.at[1], below)
 
     def dq_swap():
         return remote(dq_all.at[pl.ds(rows, rows)], dq_in, dqs_sem, dqr_sem, sibling)
@@ -195,6 +222,11 @@
         for p in range(2):
             cross_kv(p).start()
 
+    @pl.when(lender)
+    def _():
+        for i in range(2):
+            lend(i).start()
+
     def widen(x, dst, base):
         for t in range(128):
             dst[pl.ds(pl.multiple_of(base + t * heads, heads), heads), :] = jnp.broadcast_to(x[:, t:t + 1], (heads, 128))
@@ -223,6 +255,7 @@
     part[...] = jnp.zeros_like(part)
     dq_all[...] = jnp.zeros_like(dq_all)
     swap_stats().start()
+    pl.when(lender)(lambda: lend(2).start())
 
     def tiles(y, base, units, width, mask_from, c0=0):
         at = pl.ds(c0, width)
@@ -275,6 +308,43 @@
     full = 4 * (len(OFFSETS) - 1)
     end = full + 8
 
+    def help_out():
+        for i in range(3):
+            lend(i).wait_recv()
+            pass_on(i).start()
+        first = (rows - GROUP) // heads
+
+        def widen_lent(b, carry):
+            at = pl.ds(pl.multiple_of(first + b * 128, 128), 128)
+            base = 2 * rows + b * (128 * heads)
+            widen(stats[2, 0, :, at], lse_all, base)
+            widen(stats[2, 1, :, at], dl_all, base)
+            return carry
+
+        def widen_passed(b, carry):
+            at = pl.ds(pl.multiple_of(first + b * 128, 128), 128)
+            base = 2 * rows + GROUP + b * (128 * heads)
+            widen(stats[3, 0, :, at], lse_all, base)
+            widen(stats[3, 1, :, at], dl_all, base)
+            return carry
+
+        blocks = GROUP // (128 * heads)
+        lax.fori_loop(0, blocks, widen_lent, 0)
+        for i in range(3):
+            pass_on(i).wait_recv()
+        lax.fori_loop(0, blocks, widen_passed, 0)
+
+        def pieces(i, carry):
+            tiles(i % LENT, 2 * rows + (1 - i // LENT) * GROUP, UNIT, cols, None)
+            return carry
+
+        lax.fori_loop(0, LENT, pieces, 0)
+        merge().start()
+        lax.fori_loop(LENT, 2 * LENT, pieces, 0)
+        merge().wait_recv()
+        dq_all[theirs, :] += lent_dq[...]
+        give_back().start()
+
     def rows_of(j):
         return (1 - j // 2) * rows + (j % 2) * GROUP
 
@@ -282,10 +352,13 @@
         for at in SCHEDULE:
             if 0 <= at < full:
                 pl.when(t == at)(lambda: late(at))
+        pl.when(jnp.logical_and(helper, t == HELP_AT))(help_out)
         off = sum(jnp.where(t // 4 == i, o, 0) for i, o in enumerate(OFFSETS[:-1]))
         y = wrap(z + off)
 
-        @pl.when(need(z, y))
+        lent = jnp.logical_and(lender, jnp.logical_and(y < LENT, t % 2 == 1))
+
+        @pl.when(jnp.logical_and(need(z, y), jnp.logical_not(lent)))
         def _():
             tiles(y, rows_of(t % 4), UNIT, cols, None)
         return carry
@@ -320,6 +393,12 @@
     late(end + 1)
     lax.fori_loop(pairs // 2, pairs, functools.partial(diag, cols), 0)
     late(end + 2)
+
+    @pl.when(lender)
+    def _():
+        give_back().wait_recv()
+        r = pl.ds(rows - GROUP, GROUP)
+        dq_all[r, :] += lent_dq[...]
 
     dq_swap().wait_recv()
     for g in range(rows // CHUNK):
@@ -368,6 +447,18 @@
             pl.when(dn_on(e, z - 1, p))(lambda: ag_dn(e, p, e - 1).wait_send())
             pl.when(dn_on(e, z, p))(lambda: rs_up(e, p).wait_send())
     dq_swap().wait_send()
+
+    @pl.when(lender)
+    def _():
+        for i in range(3):
+            lend(i).wait_send()
+
+    @pl.when(helper)
+    def _():
+        for i in range(3):
+            pass_on(i).wait_send()
+        merge().wait_send()
+        give_back().wait_send()
 
 
 def deliver(dq, dk, dv, dq_out, dk_out, dv_out, a, b, c, sem_in, sem_out):
@@ -396,6 +487,7 @@
         flat = lambda x: x.reshape(rows, dim)
         chips = n // 2
         halves = rows // GROUP
+        held = 2 * rows + 2 * GROUP
         dma = pltpu.SemaphoreType.DMA
         hbm, vmem = pl.BlockSpec(memory_space=pl.ANY), pl.BlockSpec(memory_space=pltpu.VMEM)
         shapes = (jax.ShapeDtypeStruct((rows, dim), BF16), jax.ShapeDtypeStruct((toks, dim), BF16), jax.ShapeDtypeStruct((toks, dim), BF16))
@@ -406,22 +498,24 @@
             in_specs=[hbm] * 5 + [vmem],
             out_specs=[vmem] * 3,
             scratch_shapes=[
-                pltpu.VMEM((2 * rows, dim), BF16),
-                pltpu.VMEM((2 * rows, dim), BF16),
+                pltpu.VMEM((held, dim), BF16),
+                pltpu.VMEM((held, dim), BF16),
                 pltpu.VMEM((rows, dim), BF16),
-                pltpu.VMEM((2 * rows, 128), F32),
-                pltpu.VMEM((2 * rows, 128), F32),
-                pltpu.VMEM((2, 2, heads, toks), F32),
+                pltpu.VMEM((held, 128), F32),
+                pltpu.VMEM((held, 128), F32),
+                pltpu.VMEM((4, 2, heads, toks), F32),
                 pltpu.VMEM((chips + 1, 2, toks, dim), BF16),
                 pltpu.VMEM((chips + 1, 2, dim, toks), F32),
                 pltpu.VMEM((2, dim, toks), F32),
-                pltpu.VMEM((2 * rows, dim), F32),
+                pltpu.VMEM((held, dim), F32),
+                pltpu.VMEM((GROUP, dim), F32),
                 pltpu.VMEM((rows, dim), F32),
                 pltpu.VMEM((FAR, 2, dim, toks), F32),
                 pltpu.VMEM((FAR, 2, dim, toks), F32),
                 dma((5,)), dma((3, halves)), dma((3, halves)),
                 hops, hops, hops, hops, hops, hops, hops, hops,
                 dma, dma, dma((3,)), dma((3,)), dma((2, 2)), dma((2, 2)),
+                dma((3,)), dma((3,)), dma((3,)), dma((3,)), dma((2,)), dma((2,)),
             ],
             compiler_params=pltpu.CompilerParams(collective_id=0, has_side_effects=True, vmem_limit_bytes=60 * 2 ** 20),
         )(flat(q_tok), k_tok, v_tok, flat(fwd_out), flat(d_out), lse_row.T)

time: 103 us -> 98.2 us (0.953)
  Pallas kernels: 102 us -> 97.2 us
    pallas_call x1, Pallas kernels: 100 us -> 95 us  [local_fn(): pl.pallas_call(functools.partial(kernel, n, scale), out_shape=shapes, in_...]
where the time goes in v4:
time: 98.2 us; the launch traced here: 98 us
  Pallas kernels  97.2 us (99%)
    pallas_call x1, Pallas kernels, local_fn(): pl.pallas_call(functools.partial(kernel, n, scale), out_shape=shapes, in_...  95 us
    pallas_call x1, Pallas kernels, local_fn(): pl.pallas_call(deliver, out_shape=shapes, in_specs=[hbm] * 3, out_specs=[...  2.15 us

profile of v4, /device:TPU:30, one launch (start us, length us, event | category | flops | bytes accessed | tf_op | source)
XLA Modules:
  0.0 98.0 jit_solution(6135459399793870349)
XLA Ops:
  0.6 95.0 %shard_map.85 = (bf16[4096,128]{1,0:T(8,128)(2,1)}, bf16[512,128]{1,0:T(8,128)(2,1)}, bf16[512,128]{1,0:T(8,128)(2,1)}) custom-call(bf16[4096,128]{1,0:T(8,128)(2,1)} %bitcast.5, bf16[512,128]{1,0:T(8,128)(2,1)} %k_hbm.1, bf16[512,128]{1,0:T(8,128)(2,1)} %v_hbm.1, bf16[4096,128]{1,0:T(8,128)(2,1)} %bitcast.6, bf16[4096,128]{1,0:T(8,128)(2,1)} %bitcast.7, ...), custom_call_target="tpu_custom_call" | custom-call | tf_op jit(solution)/shard_map/pallas_call | solution.py:495
  95.7 2.1 %shard_map.86 = (bf16[4096,128]{1,0:T(8,128)(2,1)}, bf16[512,128]{1,0:T(8,128)(2,1)}, bf16[512,128]{1,0:T(8,128)(2,1)}) custom-call(bf16[4096,128]{1,0:T(8,128)(2,1)} %get-tuple-element.9.dq, bf16[512,128]{1,0:T(8,128)(2,1)} %get-tuple-element.10.dk, bf16[512,128]{1,0:T(8,128)(2,1)} %get-tuple-element.11.dv), custom_call_target="tpu_custom_call" | custom-call | tf_op jit(solution)/shard_map/pallas_call | solution.py:522

commit v5 on v4

--- a/solution.py
+++ b/solution.py
@@ -19,28 +19,26 @@
 FAR = 4
 OFFSETS = (-2, -3, -4, 3, 1, 2, -1)
 SCHEDULE = {
-    -2: (('ag', 1, 0),),
-    -1: (('ag', 1, 1),),
+    -2: (('ag', 1, 0), ('ag', 1, 1),),
     0: (('ag', 2, 0), ('ag', 2, 1),),
-    4: (('ag', 3, 0), ('ag', 3, 1),),
-    6: (('dn', 2, 0, True),),
-    7: (('ag', 4, 0),),
-    8: (('ag', 4, 1),),
-    9: (('dn', 3, 1, True),),
-    12: (('up', 4, 1, True), ('dn', 4, 0, True),),
-    14: (('dn', 3, 0, True), ('dn', 2, 1, False),),
+    3: (('ag', 3, 0), ('ag', 3, 1),),
+    6: (('ag', 4, 1),),
+    8: (('ag', 4, 0), ('dn', 3, 1, True),),
+    12: (('up', 4, 1, True), ('dn', 4, 0, True), ('dn', 3, 0, True),),
+    15: (('dn', 2, 0, True),),
     16: (('up', 3, 0, True),),
-    17: (('dn', 3, 0, False),),
-    18: (('up', 3, 1, False),),
-    23: (('dn', 2, 0, False),),
-    24: (('dn', 2, 1, True), ('up', 2, 0, False),),
-    25: (('up', 3, 1, True),),
-    27: (('up', 1, 0, True),),
-    28: (('up', 2, 1, False),),
-    29: (('dn', 1, 0, False), ('up', 2, 1, True),),
-    32: (('up', 1, 0, False), ('dn', 1, 1, False), ('dn', 1, 0, True), ('dn', 1, 1, True),),
-    33: (('up', 2, 0, True), ('up', 1, 1, False),),
-    34: (('up', 1, 1, True),),
+    18: (('dn', 3, 0, False),),
+    19: (('up', 3, 1, False),),
+    20: (('dn', 2, 1, False),),
+    23: (('dn', 2, 1, True),),
+    24: (('dn', 2, 0, False), ('up', 2, 0, False),),
+    27: (('up', 2, 1, False),),
+    28: (('dn', 1, 0, False),),
+    30: (('up', 2, 1, True), ('up', 1, 0, False),),
+    31: (('up', 2, 0, True),),
+    32: (('up', 3, 1, True), ('dn', 1, 0, True), ('dn', 1, 1, False),),
+    33: (('up', 1, 1, False), ('dn', 1, 1, True),),
+    34: (('up', 1, 1, True), ('up', 1, 0, True),),
 }
 
 
@@ -288,7 +286,6 @@
 
     late(-2)
     lax.fori_loop(0, pairs // 2, functools.partial(diag, cols // 2), 0)
-    late(-1)
     swap_stats().wait_recv()
 
     def sibling_stats(i, carry):
@@ -461,19 +458,12 @@
         give_back().wait_send()
 
 
-def deliver(dq, dk, dv, dq_out, dk_out, dv_out, a, b, c, sem_in, sem_out):
-    pieces = 4
-    step = dq.shape[0] // pieces
-    moves = [(dk, b, dk_out), (dv, c, dv_out)] + [tuple(x.at[pl.ds(i * step, step)] for x in (dq, a, dq_out)) for i in range(pieces)]
-    ins = [pltpu.make_async_copy(s, m, sem_in.at[i]) for i, (s, m, _) in enumerate(moves)]
-    outs = [pltpu.make_async_copy(m, d, sem_out.at[i]) for i, (_, m, d) in enumerate(moves)]
-    for x in ins:
-        x.start()
-    for x, o in zip(ins, outs):
-        x.wait()
-        o.start()
-    for o in outs:
-        o.wait()
+def deliver(dq, dk, dv, dq_out, dk_out, dv_out, sem):
+    moves = [pltpu.make_async_copy(s, d, sem.at[i]) for i, (s, d) in enumerate(((dq, dq_out), (dk, dk_out), (dv, dv_out)))]
+    for m in moves:
+        m.start()
+    for m in moves:
+        m.wait()
 
 
 def solution(mesh):
@@ -494,7 +484,7 @@
         hops = dma((FAR, 2))
         grads = pl.pallas_call(
             functools.partial(kernel, n, scale),
-            out_shape=shapes,
+            out_shape=tuple(pltpu.VMEM(s.shape, s.dtype) for s in shapes),
             in_specs=[hbm] * 5 + [vmem],
             out_specs=[vmem] * 3,
             scratch_shapes=[
@@ -524,8 +514,8 @@
             out_shape=shapes,
             in_specs=[hbm] * 3,
             out_specs=[hbm] * 3,
-            scratch_shapes=[pltpu.VMEM(s.shape, s.dtype) for s in shapes] + [dma((6,)), dma((6,))],
-        )(*grads)
+            scratch_shapes=[dma((3,))],
+        )(*(pltpu.with_memory_space_constraint(g, pltpu.VMEM) for g in grads))
         return dq.reshape(q_tok.shape), dk, dv
 
     return jax.shard_map(local_fn, mesh=mesh, in_specs=(row_spec,) * 6, out_specs=(row_spec,) * 3, check_vma=False)

time: 98.2 us -> 95.4 us (0.971)
  Pallas kernels: 97.2 us -> 94.5 us
    pallas_call x1, Pallas kernels: 95 us -> 93.4 us  [local_fn(): pl.pallas_call(functools.partial(kernel, n, scale), out_shape=tuple((pltp...]
    pallas_call x1, Pallas kernels: 2.15 us -> 1.07 us  [local_fn(): pl.pallas_call(deliver, out_shape=shapes, in_specs=[hbm] * 3, out_specs=[...]
where the time goes in v5:
time: 95.4 us; the launch traced here: 95.3 us
  Pallas kernels  94.5 us (99%)
    pallas_call x1, Pallas kernels, local_fn(): pl.pallas_call(functools.partial(kernel, n, scale), out_shape=tuple((pltp...  93.4 us

profile of v5, /device:TPU:30, one launch (start us, length us, event | category | flops | bytes accessed | tf_op | source)
XLA Modules:
  0.0 95.3 jit_solution(4439625144778793639)
XLA Ops:
  0.6 93.4 %shard_map.85 = (bf16[4096,128]{1,0:T(8,128)(2,1)S(1)}, bf16[512,128]{1,0:T(8,128)(2,1)S(1)}, bf16[512,128]{1,0:T(8,128)(2,1)S(1)}) custom-call(bf16[4096,128]{1,0:T(8,128)(2,1)} %bitcast.5, bf16[512,128]{1,0:T(8,128)(2,1)} %k_hbm.1, bf16[512,128]{1,0:T(8,128)(2,1)} %v_hbm.1, bf16[4096,128]{1,0:T(8,128)(2,1)} %bitcast.6, bf16[4096,128]{1,0:T(8,128)(2,1)} %bitcast.7, ...), custom_call_target="tpu_custom_call" | custom-call | tf_op jit(solution)/shard_map/pallas_call | solution.py:485
  94.0 1.1 %shard_map.86 = (bf16[4096,128]{1,0:T(8,128)(2,1)}, bf16[512,128]{1,0:T(8,128)(2,1)}, bf16[512,128]{1,0:T(8,128)(2,1)}) custom-call(bf16[4096,128]{1,0:T(8,128)(2,1)S(1)} %get-tuple-element.9.dq, bf16[512,128]{1,0:T(8,128)(2,1)S(1)} %get-tuple-element.10.dk, bf16[512,128]{1,0:T(8,128)(2,1)S(1)} %get-tuple-element.11.dv), custom_call_target="tpu_custom_call" | custom-call | tf_op jit(solution)/shard_map/pallas_call | solution.py:512
